TPU v7x, 32 devices: a whole 2x2x4 slice. The times are simulated.
32 devices in a mesh: rep: 2 (over x), tp: 4 (over z), dp: 4 (over y, core).
Axes of the slice: x: 2, y: 2, z: 4, core: 2. Of those that a mesh axis runs over, the one named last changes fastest.
Arguments:
- grad_partial: float32 [8, 4, 1024, 4096], P(('rep', 'dp'), None, None, 'tp'), parts along dimension 0
- momentum: float32 [8, 1024, 4096], P('rep', 'dp', 'tp'), parts along dimension 0
- weight: float32 [8, 1024, 4096], P('rep', 'dp', 'tp'), parts along dimension 0
- learn_rate: float32 [8], P('rep'), parts along dimension 0
- decay_rate: float32 [], replicated
Outputs:
- output 1: float32 [8, 1024, 4096], P('rep', 'dp', 'tp'), parts along dimension 0
- output 2: float32 [8, 1024, 4096], P('rep', 'dp', 'tp'), parts along dimension 0
- output 3: bfloat16 [8, 1024, 4096], P('rep', None, 'tp'), parts along dimension 0
There are 2 independent parts. A program takes and returns all parts, laid end to end along the dimension named above; an argument that names none is the same for every part.
All inputs are finite; a program needn't handle non-finite values.
Results may differ from a plain program's by a relative error of at most 0.0110385.
Values are sent between devices in bfloat16 or wider.
A program may use at most 1 GiB of HBM per device.

v0:
```python
import math
import jax
import jax.numpy as jnp
from jax import lax
from jax.sharding import PartitionSpec as P, NamedSharding

MOMENTUM = 0.95
NS_STEPS = 5
COEF_A = 3.4445
COEF_B = -4.7750
COEF_C = 2.0315
NORM_EPS = 1e-7


def newton_schulz(update, short_rows):
    upd_f32 = update.astype(jnp.float32)
    norm_val = jnp.sqrt(jnp.sum(upd_f32 * upd_f32, axis=(1, 2), keepdims=True))
    x_cur = (upd_f32 / (norm_val + NORM_EPS)).astype(jnp.bfloat16)
    for step_idx in range(NS_STEPS):
        if short_rows:
            gram_mat = jnp.einsum("bik,bjk->bij", x_cur, x_cur, preferred_element_type=jnp.float32)
        else:
            gram_mat = jnp.einsum("bki,bkj->bij", x_cur, x_cur, preferred_element_type=jnp.float32)
        gram_mat = gram_mat.astype(jnp.bfloat16)
        gram_sq = jnp.einsum("bij,bjk->bik", gram_mat, gram_mat, preferred_element_type=jnp.float32)
        poly_mat = (COEF_B * gram_mat.astype(jnp.float32) + COEF_C * gram_sq).astype(jnp.bfloat16)
        if short_rows:
            prod_mat = jnp.einsum("bij,bjk->bik", poly_mat, x_cur, preferred_element_type=jnp.float32)
        else:
            prod_mat = jnp.einsum("bkj,bij->bki", x_cur, poly_mat, preferred_element_type=jnp.float32)
        x_cur = (COEF_A * x_cur.astype(jnp.float32) + prod_mat).astype(jnp.bfloat16)
    return x_cur


def solution(mesh):
    dp_size = mesh.shape["dp"]
    tp_size = mesh.shape["tp"]

    def local_step(grad_local, mom_local, weight_local, learn_rate, decay_rate):
        grad_sum = lax.psum_scatter(grad_local[0], "dp", scatter_dimension=1, tiled=True)
        grad_mean = grad_sum / dp_size
        mom_new = MOMENTUM * mom_local + grad_mean
        update = (grad_mean + MOMENTUM * mom_new).astype(jnp.bfloat16)
        whole_rows = lax.all_to_all(update, "dp", split_axis=0, concat_axis=1, tiled=True)
        whole_mats = lax.all_gather(whole_rows, "tp", axis=2, tiled=True)
        row_count = whole_mats.shape[1]
        col_count = whole_mats.shape[2]
        ortho_mat = newton_schulz(whole_mats, row_count <= col_count)
        col_width = col_count // tp_size
        own_cols = lax.dynamic_slice_in_dim(ortho_mat, lax.axis_index("tp") * col_width, col_width, axis=2)
        ortho_rows = lax.all_to_all(own_cols, "dp", split_axis=1, concat_axis=0, tiled=True)
        out_scale = 0.2 * math.sqrt(max(row_count, col_count))
        rate_col = learn_rate[:, None, None]
        weight_new = weight_local - rate_col * (out_scale * ortho_rows.astype(jnp.float32) + decay_rate * weight_local)
        weight_full = lax.all_gather(weight_new.astype(jnp.bfloat16), "dp", axis=1, tiled=True)
        return mom_new, weight_new, weight_full

    return jax.shard_map(
        local_step,
        mesh=mesh,
        in_specs=(P(("rep", "dp"), None, None, "tp"), P("rep", "dp", "tp"), P("rep", "dp", "tp"), P("rep"), P()),
        out_specs=(P("rep", "dp", "tp"), P("rep", "dp", "tp"), P("rep", None, "tp")),
        check_vma=False,
    )
```

profile of v0, /device:TPU:0, one launch (start us, length us, event | category | flops | bytes accessed | tf_op | source)
XLA Modules:
  0.0 643.1 jit_solution(17269042898608159178)
XLA Ops:
  7.2 0.0 reduce-scatter.2.cloned.1.call-start
  7.2 0.7 reduce-scatter.2.cloned.1.call-update
  7.9 0.0 all-gather.3.cloned.1.call-start
  7.9 129.7 %reduce-scatter.2.cloned.1.call-done = f32[4,256,1024]{2,1,0:T(8,128)} async-done(((f32[4,1024,1024]{2,1,0:T(8,128)}), f32[4,256,1024]{2,1,0:T(8,128)}) %reduce-scatter.2.cloned.1.call-update) | async-done | bytes 4194320 | tf_op jit(solution)/shard_map/reduce_scatter | solution.py:40
  137.6 7.1 %add_convert_fusion.5 = (bf16[4,256,1024]{2,1,0:T(8,128)(2,1)S(1)}, f32[4,256,1024]{2,1,0:T(8,128)}) fusion(f32[4,256,1024]{2,1,0:T(8,128)} %reduce-scatter.2.cloned.1.call-done, f32[4,256,1024]{2,1,0:T(8,128)} %param.6), kind=kLoop, calls=%fused_computation.37 | loop fusion | flops 6291456 | bytes 14680064 | tf_op jit(solution)/shard_map/convert_element_type | solution.py:43
  144.8 28.8 %all_to_all.21 = bf16[4,256,1024]{2,1,0:T(8,128)(2,1)} all-to-all(bf16[4,256,1024]{2,1,0:T(8,128)(2,1)S(1)} %get-tuple-element.5), channel_id=1, replica_groups=mesh['rep'=2,'tp'=4,'dp'=4] {'dp'}, dimensions={0} | all-to-all | bytes 4194304 | tf_op jit(solution)/shard_map/all_to_all | solution.py:44
  173.6 0.0 all-gather.3.cloned.1.call-update
  173.6 149.7 %all-gather.3.cloned.1.call-done = bf16[1,1024,4096]{2,1,0:T(8,128)(2,1)} async-done(((bf16[1,1024,1024]{2,1,0:T(8,128)(2,1)}), bf16[1,1024,4096]{2,1,0:T(8,128)(2,1)}) %all-gather.3.cloned.1.call-update) | async-done | bytes 8388624 | tf_op jit(solution)/shard_map/all_gather | solution.py:45
  323.3 8.3 %fusion = f32[]{:T(128)} fusion(bf16[1,1024,4096]{2,1,0:T(8,128)(2,1)} %all-gather.3.cloned.1.call-done), kind=kLoop, calls=%fused_computation.2 | loop fusion | flops 12582911 | bytes 8388612 | tf_op jit(solution)/shard_map/reduce_sum | solution.py:17
  332.2 14.7 %fusion.19 = bf16[1024,1024]{1,0:T(8,128)(2,1)S(1)} fusion(bf16[1,1024,4096]{2,1,0:T(8,128)(2,1)} %all-gather.3.cloned.1.call-done, f32[]{:T(128)S(6)} %add.55), kind=kOutput, calls=%fused_computation.26 | convolution fusion | flops 8602517504 | bytes 10485764 | tf_op jit(solution)/shard_map/bik,bjk->bij/dot_general | solution.py:21
  346.9 19.2 %fusion.5 = bf16[1,1024,4096]{2,1,0:T(8,128)(2,1)} fusion(bf16[1024,1024]{1,0:T(8,128)(2,1)S(1)} %fusion.19, f32[]{:T(128)S(6)} %add.55, bf16[1,1024,4096]{2,1,0:T(8,128)(2,1)} %all-gather.3.cloned.1.call-done), kind=kOutput, calls=%fused_computation.11 | convolution fusion | flops 10784604160 | bytes 18874372 | tf_op jit(solution)/shard_map/bij,bjk->bik/dot_general | solution.py:28
  366.1 14.9 %fusion.16 = bf16[1024,1024]{1,0:T(8,128)(2,1)S(1)} fusion(bf16[1,1024,4096]{2,1,0:T(8,128)(2,1)} %fusion.5), kind=kOutput, calls=%fused_computation.23 | convolution fusion | flops 8589934592 | bytes 10485760 | tf_op jit(solution)/shard_map/bik,bjk->bij/dot_general | solution.py:21
  381.0 18.9 %fusion.4 = bf16[1,1024,4096]{2,1,0:T(8,128)(2,1)} fusion(bf16[1,1024,4096]{2,1,0:T(8,128)(2,1)} %fusion.5, bf16[1024,1024]{1,0:T(8,128)(2,1)S(1)} %fusion.16), kind=kOutput, calls=%fused_computation.9 | convolution fusion | flops 10759438336 | bytes 18874368 | tf_op jit(solution)/shard_map/bij,bjk->bik/dot_general | solution.py:28
  399.9 14.6 %fusion.13 = bf16[1024,1024]{1,0:T(8,128)(2,1)S(1)} fusion(bf16[1,1024,4096]{2,1,0:T(8,128)(2,1)} %fusion.4), kind=kOutput, calls=%fused_computation.20 | convolution fusion | flops 8589934592 | bytes 10485760 | tf_op jit(solution)/shard_map/bik,bjk->bij/dot_general | solution.py:21
  414.6 19.3 %fusion.3 = bf16[1,1024,4096]{2,1,0:T(8,128)(2,1)} fusion(bf16[1,1024,4096]{2,1,0:T(8,128)(2,1)} %fusion.4, bf16[1024,1024]{1,0:T(8,128)(2,1)S(1)} %fusion.13), kind=kOutput, calls=%fused_computation.7 | convolution fusion | flops 10759438336 | bytes 18874368 | tf_op jit(solution)/shard_map/bij,bjk->bik/dot_general | solution.py:28
  433.8 14.7 %fusion.10 = bf16[1024,1024]{1,0:T(8,128)(2,1)S(1)} fusion(bf16[1,1024,4096]{2,1,0:T(8,128)(2,1)} %fusion.3), kind=kOutput, calls=%fused_computation.17 | convolution fusion | flops 8589934592 | bytes 10485760 | tf_op jit(solution)/shard_map/bik,bjk->bij/dot_general | solution.py:21
  448.5 19.1 %fusion.2 = bf16[1,1024,4096]{2,1,0:T(8,128)(2,1)} fusion(bf16[1,1024,4096]{2,1,0:T(8,128)(2,1)} %fusion.3, bf16[1024,1024]{1,0:T(8,128)(2,1)S(1)} %fusion.10), kind=kOutput, calls=%fused_computation.5 | convolution fusion | flops 10759438336 | bytes 18874368 | tf_op jit(solution)/shard_map/bij,bjk->bik/dot_general | solution.py:28
  467.6 14.6 %fusion.7 = bf16[1024,1024]{1,0:T(8,128)(2,1)S(1)} fusion(bf16[1,1024,4096]{2,1,0:T(8,128)(2,1)} %fusion.2), kind=kOutput, calls=%fused_computation.14 | convolution fusion | flops 8589934592 | bytes 10485760 | tf_op jit(solution)/shard_map/bik,bjk->bij/dot_general | solution.py:21
  482.3 18.1 %convolution_bitcast_fusion = f32[1,1024,4096]{2,1,0:T(8,128)} fusion(bf16[1,1024,4096]{2,1,0:T(8,128)(2,1)} %fusion.2, bf16[1024,1024]{1,0:T(8,128)(2,1)S(1)} %fusion.7), kind=kOutput, calls=%fused_computation.12 | convolution fusion | flops 10742661120 | bytes 27262976 | tf_op jit(solution)/shard_map/bij,bjk->bik/dot_general | solution.py:28
  500.4 3.7 fusion.21
  504.0 5.2 copy.11
  509.3 0.5 broadcast.81
  509.8 12.8 %reduce.1 = bf16[1024,1024]{1,0:T(8,128)(2,1)S(1)} reduce(bf16[1024,1,1024]{2,1,0:T(2,128)(2,1)} %bitcast.61, bf16[]{:T(256)} %broadcast.81), dimensions={1}, to_apply=%bitcast.60.reduce_sub_computation | reduce | bytes 4194306
  522.6 2.8 reshape.129
  525.3 3.6 all-to-all-start.1
  529.0 0.0 all-gather.5.cloned.1.call-start
  529.7 24.7 %all-to-all-done.1 = bf16[4,2,131072]{2,1,0:T(2,128)(2,1)S(1)} async-done(((bf16[4,2,131072]{2,1,0:T(2,128)(2,1)}), bf16[4,2,131072]{2,1,0:T(2,128)(2,1)S(1)}, u32[]{:S(2)}, u32[]{:S(2)}) %all-to-all-start.1) | async-done | bytes 2097184 | tf_op jit(solution)/shard_map/all_to_all | solution.py:51
  554.4 3.5 reshape.130
  557.9 7.9 %convert_multiply_fusion.1 = f32[1,1024,1024]{2,0,1:T(1,128)S(1)} fusion(bf16[1024,1,1024]{2,1,0:T(2,128)(2,1)} %reshape.130), kind=kLoop, calls=%fused_computation.31 | loop fusion | flops 2097152 | bytes 6291456 | tf_op jit(solution)/shard_map/mul | solution.py:54
  565.8 0.0 copy-start
  565.9 0.0 copy-start.1
  565.9 1.0 copy.9
  566.9 1.1 copy-done
  568.0 0.0 copy-done.1
  568.0 4.1 fusion.54
  572.2 0.0 all-gather.5.cloned.1.call-update
  572.2 56.2 %all-gather.5.cloned.1.call-done = bf16[4,1024,1024]{2,1,0:T(8,128)(2,1)} async-done(((bf16[4,256,1024]{2,1,0:T(8,128)(2,1)}), bf16[4,1024,1024]{2,1,0:T(8,128)(2,1)}) %all-gather.5.cloned.1.call-update) | async-done | bytes 8388624 | tf_op jit(solution)/shard_map/all_gather | solution.py:55
  628.4 7.8 %copy.14 = bf16[4,1024,1024]{2,1,0:T(8,128)(2,1)} copy(bf16[4,1024,1024]{2,1,0:T(8,128)(2,1)} %all-gather.5.cloned.1.call-done) | data formatting | bytes 16777216
Async XLA Ops:
  7.2 130.5 %reduce-scatter.2.cloned.1.call-start = ((), (), s32[]{:S(2)}) async-start(), calls=%async_computation.3 | async-start | bytes 20971520 | tf_op jit(solution)/shard_map/reduce_scatter | solution.py:40
  7.9 315.4 %all-gather.3.cloned.1.call-start = ((), (), s32[]{:S(2)}) async-start(), calls=%async_computation.4 | async-start | bytes 10485760 | tf_op jit(solution)/shard_map/all_gather | solution.py:45
  525.3 29.0 %all-to-all-start.1 = ((bf16[4,2,131072]{2,1,0:T(2,128)(2,1)}), bf16[4,2,131072]{2,1,0:T(2,128)(2,1)S(1)}, u32[]{:S(2)}, u32[]{:S(2)}) async-start(bf16[4,2,131072]{2,1,0:T(2,128)(2,1)} %reshape.129), calls=%async_computation.2 | async-start | bytes 4194304 | tf_op jit(solution)/shard_map/all_to_all | solution.py:51
  529.0 99.4 %all-gather.5.cloned.1.call-start = ((), (), s32[]{:S(2)}) async-start(), calls=%async_computation.5 | async-start | bytes 10485760 | tf_op jit(solution)/shard_map/all_gather | solution.py:55
  565.8 2.2 copy-start
  565.9 2.2 copy-start.1
Sparse Core Ops, SparseCore 0:
  10.5 127.0 reduce-scatter.1
  173.7 149.4 all-gather.2
  572.3 55.9 all-gather.4
where the time goes:
time: 653 us; the launch traced here: 643 us
  waiting for transfers between devices  361 us (55%)
  matrix products  168 us (26%)
  other arithmetic  43.9 us (7%)
  blocking collectives  28.8 us (4%)
  local copies, waits for them, and re-layouts  22 us (3%)
  between operations  15.6 us (2%)
    all_gather x1, waiting for transfers between devices, local_step(): whole_mats = lax.all_gather(whole_rows, 'tp', axis=2, tiled=True)  150 us
    reduce_scatter x1, waiting for transfers between devices, local_step(): lax.psum_scatter(grad_local[0], 'dp', scatter_dimension=1, tiled=True)  130 us
    dot_general x5, matrix products, newton_schulz(): jnp.einsum('bij,bjk->bik', poly_mat, x_cur, preferred_element_type=jnp.fl...  94.6 us
    dot_general x5, matrix products, newton_schulz(): jnp.einsum('bik,bjk->bij', x_cur, x_cur, preferred_element_type=jnp.float32)  73.5 us
    all_gather x1, waiting for transfers between devices, local_step(): lax.all_gather(weight_new.astype(jnp.bfloat16), 'dp', axis=1, tiled=True)  56.2 us
    all_to_all x1, blocking collectives, local_step(): lax.all_to_all(update, 'dp', split_axis=0, concat_axis=1, tiled=True)  28.8 us
    all_to_all x1, waiting for transfers between devices, local_step(): lax.all_to_all(own_cols, 'dp', split_axis=1, concat_axis=0, tiled=True)  24.7 us
    unnamed x9, local copies, waits for them, and re-layouts  16.7 us
  transfers between devices with their start and end apart: 4, of which 4 were waited for; matrix products, arithmetic and copies ran while one was open for 0% of the time, Pallas kernels for 0%

commit v1 on v0

v1 whole, which is shorter than its diff:
```python
import functools
import math

import jax
import jax.numpy as jnp
from jax import lax
from jax.experimental import pallas as pl
from jax.experimental.pallas import tpu as pltpu
from jax.sharding import PartitionSpec as P

MOMENTUM = 0.95
NS_STEPS = 5
COEF_A = 3.4445
COEF_B = -4.7750
COEF_C = 2.0315
NORM_EPS = 1e-7

MATS = 4
DP = 4
TP = 4
HALVES = 2
F32 = jnp.float32
BF16 = jnp.bfloat16
NT = (((1,), (1,)), ((), ()))

ORDER = [(0, 0), (2, 0), (0, 1), (2, 1), (1, 0), (3, 0), (1, 1), (3, 1)]


def mesh_copy(src, dst, send, recv, **axes):
    return pltpu.make_async_remote_copy(
        src_ref=src, dst_ref=dst, send_sem=send, recv_sem=recv,
        device_id=axes, device_id_type=pl.DeviceIdType.MESH)


def relations():
    me = lax.axis_index("dp")
    y, c = lax.div(me, 2), lax.rem(me, 2)
    return me, 2 * y + (1 - c), 2 * (1 - y) + c, 2 * (1 - y) + (1 - c)


def front_kernel(grad, mom, mom_new, ub_out,
                 own_yp, own_me, recv_a, recv_b, recv_y, momb, ub, xg,
                 ld_yp, ld_me, ld_mom, sa, ra, sb, rb, sy, ry, su, ru, zr, zsr, zsl, so, sm):
    me, partner, yp, diag = relations()
    z = lax.axis_index("tp")
    nchunk = len(ORDER)
    half = own_me.shape[1]
    rows = HALVES * half

    barrier = pltpu.get_barrier_semaphore()
    for peer in (partner, yp, diag):
        pl.semaphore_signal(barrier, inc=1, device_id={"dp": peer}, device_id_type=pl.DeviceIdType.MESH)

    @pl.when(z > 0)
    def _():
        pl.semaphore_signal(barrier, inc=1, device_id={"tp": z - 1}, device_id_type=pl.DeviceIdType.MESH)

    @pl.when(z < TP - 1)
    def _():
        pl.semaphore_signal(barrier, inc=1, device_id={"tp": z + 1}, device_id_type=pl.DeviceIdType.MESH)

    def load_yp(k):
        m, h = ORDER[k]
        return pltpu.make_async_copy(grad.at[0, m, pl.ds(yp * rows + h * half, half), :], own_yp.at[k], ld_yp.at[k])

    def load_me(k):
        m, h = ORDER[k]
        return pltpu.make_async_copy(grad.at[0, m, pl.ds(me * rows + h * half, half), :], own_me.at[k], ld_me.at[k])

    def load_mom(k):
        m, h = ORDER[k]
        return pltpu.make_async_copy(mom.at[m, pl.ds(h * half, half), :], momb.at[k], ld_mom.at[k])

    def copy_a(k):
        m, h = ORDER[k]
        return mesh_copy(grad.at[0, m, pl.ds(diag * rows + h * half, half), :], recv_a.at[k], sa.at[k], ra.at[k], dp=partner)

    def copy_b(k):
        m, h = ORDER[k]
        return mesh_copy(grad.at[0, m, pl.ds(partner * rows + h * half, half), :], recv_b.at[k], sb.at[k], rb.at[k], dp=partner)

    def copy_y(k):
        return mesh_copy(own_yp.at[k], recv_y.at[k], sy.at[k], ry.at[k], dp=yp)

    def store_mom(k):
        m, h = ORDER[k]
        return pltpu.make_async_copy(momb.at[k], mom_new.at[m, pl.ds(h * half, half), :], sm.at[k])

    def chunk_rows(r, h):
        return pl.ds(pl.multiple_of(r * rows + h * half, half), half)

    def copy_u(k):
        m, h = ORDER[k]
        return mesh_copy(ub.at[k], xg.at[z, chunk_rows(me, h), :], su.at[k], ru.at[me, h], dp=m)

    for k in range(nchunk):
        load_yp(k).start()
    for k in range(nchunk):
        load_me(k).start()
        load_mom(k).start()
    pl.semaphore_wait(barrier, 3 + jnp.where(z > 0, 1, 0) + jnp.where(z < TP - 1, 1, 0))
    for k in range(nchunk):
        copy_a(k).start()
    for k in range(nchunk):
        copy_b(k).start()

    def chip_sum(k):
        load_yp(k).wait()
        copy_a(k).wait_recv()

        @pl.loop(0, half // 32)
        def _(i):
            sl = pl.ds(pl.multiple_of(i * 32, 32), 32)
            own_yp[k, sl, :] = own_yp[k, sl, :] + recv_a[k, sl, :]

    def update_chunk(k):
        m, h = ORDER[k]
        load_me(k).wait()
        copy_b(k).wait_recv()
        load_mom(k).wait()
        copy_y(k).wait_recv()

        @pl.loop(0, half // 32)
        def _(i):
            sl = pl.ds(pl.multiple_of(i * 32, 32), 32)
            g = (own_me[k, sl, :] + recv_b[k, sl, :] + recv_y[k, sl, :]) * (1.0 / DP)
            mn = MOMENTUM * momb[k, sl, :] + g
            momb[k, sl, :] = mn
            ub[k, sl, :] = (g + MOMENTUM * mn).astype(BF16)

        @pl.when(me == m)
        def _():
            xg[z, chunk_rows(m, h), :] = ub[k]

        @pl.when(me != m)
        def _():
            copy_u(k).start()

        store_mom(k).start()

    chunks = [(h, i) for h in range(HALVES) for i in range(DP)]
    peer_of = (me, partner, yp, diag)

    def z_rows(q):
        h, i = chunks[q]
        return chunk_rows(peer_of[i], h)

    def z_right(q, s):
        return mesh_copy(xg.at[s, z_rows(q), :], xg.at[s, z_rows(q), :], zsr.at[s, q], zr.at[s, q], tp=z + 1)

    def z_left(q, s):
        return mesh_copy(xg.at[s, z_rows(q), :], xg.at[s, z_rows(q), :], zsl.at[s, q], zr.at[s, q], tp=z - 1)

    def z_out(q, s):
        return pltpu.make_async_copy(xg.at[s, z_rows(q), :], ub_out.at[s, z_rows(q), :], so.at[s, q])

    def z_own(q):
        h, i = chunks[q]
        if i > 0:
            r = peer_of[i]
            mesh_copy(ub.at[0], xg.at[z, chunk_rows(r, h), :], su.at[0], ru.at[r, h], dp=r).wait_recv()

        @pl.when(z < TP - 1)
        def _():
            z_right(q, z).start()

        @pl.when(z > 0)
        def _():
            z_left(q, z).start()

        z_out(q, z).start()

    def z_forward(q, step):
        @pl.when(z - step >= 0)
        def _():
            z_left(q, z - step).wait_recv()

            @pl.when(z < TP - 1)
            def _():
                z_right(q, z - step).start()

            z_out(q, z - step).start()

        @pl.when(z + step < TP)
        def _():
            z_left(q, z + step).wait_recv()

            @pl.when(z > 0)
            def _():
                z_left(q, z + step).start()

            z_out(q, z + step).start()

    def z_stage(t):
        nq = len(chunks)
        if t < nq:
            z_own(t)
        for step in range(1, TP):
            if 0 <= t - step < nq:
                z_forward(t - step, step)

    early = {1: (0, 1), 2: (2, 3), 3: (4, 5), 4: (6, 7), 5: (8, 9, 10)}
    late = {5: (0, 1), 6: (2, 3), 7: (4, 5, 6, 7, 8, 9, 10)}

    chip_sum(0)
    chip_sum(1)
    copy_y(0).start()
    copy_y(1).start()
    for k in range(nchunk):
        if k + 2 < nchunk:
            chip_sum(k + 2)
        update_chunk(k)
        if k + 2 < nchunk:
            copy_y(k + 2).start()
        if k in early:
            @pl.when(lax.rem(me, 2) == 0)
            def _():
                for t in early[k]:
                    z_stage(t)
        if k in late:
            @pl.when(lax.rem(me, 2) == 1)
            def _():
                for t in late[k]:
                    z_stage(t)

    for k in range(nchunk):
        copy_a(k).wait_send()
        copy_b(k).wait_send()
        copy_y(k).wait_send()
        store_mom(k).wait()

        @pl.when(me != ORDER[k][0])
        def _():
            copy_u(k).wait_send()
    for q in range(len(chunks)):
        for s in range(TP):
            z_out(q, s).wait()

            @pl.when(jnp.logical_and(s <= z, z < TP - 1))
            def _():
                z_right(q, s).wait_send()

            @pl.when(jnp.logical_and(s >= z, z > 0))
            def _():
                z_left(q, s).wait_send()


def front(grad, mom):
    _, mats, all_rows, cols = grad.shape
    rows = mom.shape[1]
    half = rows // HALVES
    n = len(ORDER)
    dma = pltpu.SemaphoreType.DMA
    buf = pltpu.VMEM((n, half, cols), F32)
    return pl.pallas_call(
        front_kernel,
        out_shape=(jax.ShapeDtypeStruct(mom.shape, F32), jax.ShapeDtypeStruct((TP, all_rows, cols), BF16)),
        in_specs=[pl.BlockSpec(memory_space=pl.ANY)] * 2,
        out_specs=[pl.BlockSpec(memory_space=pl.ANY)] * 2,
        scratch_shapes=[buf] * 6 + [pltpu.VMEM((n, half, cols), BF16), pltpu.VMEM((TP, all_rows, cols), BF16)]
        + [dma((n,))] * 10 + [dma((DP, HALVES))] + [dma((TP, n))] * 4 + [dma((n,))],
        compiler_params=pltpu.CompilerParams(collective_id=0, has_side_effects=True, vmem_limit_bytes=60 * 2**20),
        name="front",
    )(grad, mom)


def dot(a, b):
    return jnp.dot(a, b, preferred_element_type=F32)


def ortho_kernel(u, out, x, gram, poly):
    size, width = x.shape
    part = width // TP
    block = 256
    nblk = size // block

    def square_sum(i, acc):
        sl = pl.ds(pl.multiple_of(i * 16, 16), 16)
        for s in range(TP):
            v = u[s, sl, :].astype(F32)
            acc = acc + v * v
        return acc

    total = lax.fori_loop(0, size // 16, square_sum, jnp.zeros((16, part), F32))
    inv = 1.0 / (jnp.sqrt(jnp.sum(total, keepdims=True)) + NORM_EPS)

    @pl.loop(0, size // 16)
    def _(i):
        sl = pl.ds(pl.multiple_of(i * 16, 16), 16)
        for s in range(TP):
            x[sl, s * part:(s + 1) * part] = (u[s, sl, :].astype(F32) * inv).astype(BF16)

    def make_poly():
        for i in range(nblk):
            for j in range(i, nblk):
                blk = lax.dot_general(x[i * block:(i + 1) * block, :], x[j * block:(j + 1) * block, :], NT,
                                      preferred_element_type=F32).astype(BF16)
                gram[i * block:(i + 1) * block, j * block:(j + 1) * block] = blk
                if j > i:
                    gram[j * block:(j + 1) * block, i * block:(i + 1) * block] = blk.T
        poly[...] = (COEF_B * gram[...].astype(F32) + COEF_C * dot(gram[...], gram[...])).astype(BF16)

    @pl.loop(0, NS_STEPS - 1)
    def _(step):
        make_poly()

        @pl.loop(0, TP)
        def _(t):
            cs = pl.ds(pl.multiple_of(t * part, part), part)
            xc = x[:, cs]
            x[:, cs] = (COEF_A * xc.astype(F32) + dot(poly[...], xc)).astype(BF16)

    make_poly()
    xc = x[:, pl.ds(pl.multiple_of(lax.axis_index("tp") * part, part), part)]
    out[...] = (COEF_A * xc.astype(F32) + dot(poly[...], xc)).astype(BF16)


def ortho(ub):
    tp, size, part = ub.shape
    width = tp * part
    flops = 2 * size * size * (2 * width + size) * NS_STEPS
    return pl.pallas_call(
        ortho_kernel,
        out_shape=jax.ShapeDtypeStruct((size, part), BF16),
        in_specs=[pl.BlockSpec(memory_space=pltpu.VMEM)],
        out_specs=pl.BlockSpec(memory_space=pltpu.VMEM),
        scratch_shapes=[pltpu.VMEM((size, width), BF16), pltpu.VMEM((size, size), BF16), pltpu.VMEM((size, size), BF16)],
        compiler_params=pltpu.CompilerParams(vmem_limit_bytes=56 * 2**20),
        cost_estimate=pl.CostEstimate(flops=flops, bytes_accessed=2 * size * width, transcendentals=0),
        name="ortho",
    )(ub)


def tail_kernel(out_scale, x5, wg_p, wg_yp, wg_diag, weight, lr, decay,
                w_new, wb,
                xv, wgv, wv, xr, ws, wo, wn,
                lx, lg, lw, sx, rx, sw, swy, ry, rd, sd, sf, sl_b, sl_n):
    me, partner, yp, diag = relations()
    rows = weight.shape[1]
    peers = (me, partner, yp, diag)

    barrier = pltpu.get_barrier_semaphore()
    for peer in peers[1:]:
        pl.semaphore_signal(barrier, inc=1, device_id={"dp": peer}, device_id_type=pl.DeviceIdType.MESH)

    def block(r):
        return pl.ds(pl.multiple_of(r * rows, rows), rows)

    load_g = [pltpu.make_async_copy(ref, wgv.at[i], lg.at[i]) for i, ref in enumerate((wg_p, wg_yp, wg_diag))]
    load_x = [pltpu.make_async_copy(x5.at[block(peers[i]), :], xv.at[i], lx.at[i]) for i in range(DP)]
    load_w = [pltpu.make_async_copy(weight.at[peers[i]], wv.at[i], lw.at[i]) for i in range(DP)]
    for c in load_x + load_w + load_g:
        c.start()
    pl.semaphore_wait(barrier, 3)

    send_x = [mesh_copy(x5.at[block(peers[i]), :], xr.at[me], sx.at[i], rx.at[me], dp=peers[i]) for i in range(1, DP)]
    for c in (send_x[1], send_x[2], send_x[0]):
        c.start()

    def apply(w, x, mat):
        return w - lr[mat] * (out_scale * x.astype(F32) + decay[0] * w)

    def each(fn):
        @pl.loop(0, rows // 32)
        def _(i):
            fn(pl.ds(pl.multiple_of(i * 32, 32), 32))

    def to_partner(src, mat, r, sem):
        return mesh_copy(src, wb.at[mat, block(r), :], sem, rd.at[mat, r], dp=partner)

    local_b = []
    own_sends = []
    for i in range(DP):
        load_x[i].wait()
        if i == 0:
            load_w[0].wait()

            def own(sl):
                w = apply(wv[0, sl, :], xv[0, sl, :], me)
                wn[0, sl, :] = w
                ws[0, sl, :] = w.astype(BF16)
            each(own)
            c = pltpu.make_async_copy(wn.at[0], w_new.at[me], sl_n.at[0])
            c.start()
            local_b.append(c)
        else:
            load_g[i - 1].wait()

            def other(sl, i=i):
                ws[i, sl, :] = apply(wgv[i - 1, sl, :], xv[i, sl, :], me).astype(BF16)
            each(other)
        if i < 2:
            c = mesh_copy(ws.at[i], wb.at[me, block(peers[i]), :], swy.at[i], ry.at[me], dp=peers[2 + i])
            c.start()
            own_sends.append(c)
        if i != 1:
            c = to_partner(ws.at[i], me, peers[i], sd.at[i])
            c.start()
            own_sends.append(c)
        c = pltpu.make_async_copy(ws.at[i], wb.at[me, block(peers[i]), :], sl_b.at[i])
        c.start()
        local_b.append(c)

    for i in range(1, DP):
        load_w[i].wait()
        mesh_copy(x5.at[block(me), :], xr.at[peers[i]], sx.at[0], rx.at[peers[i]], dp=peers[i]).wait_recv()

        def rest(sl, i=i):
            w = apply(wv[i, sl, :], xr[peers[i], sl, :], peers[i])
            wn[i, sl, :] = w
            wo[i, sl, :] = w.astype(BF16)
        each(rest)
        if i > 1:
            c = to_partner(wo.at[i], peers[i], me, sw.at[i])
            c.start()
            own_sends.append(c)
        for c in (pltpu.make_async_copy(wn.at[i], w_new.at[peers[i]], sl_n.at[i]),
                  pltpu.make_async_copy(wo.at[i], wb.at[peers[i], block(me), :], sl_b.at[DP + i])):
            c.start()
            local_b.append(c)

    for i in (2, 3):
        dst = wb.at[peers[i], block(yp), :]
        mesh_copy(ws.at[0], dst, swy.at[0], ry.at[peers[i]], dp=peers[i]).wait_recv()
        c = to_partner(dst, peers[i], yp, sf.at[i])
        c.start()
        own_sends.append(c)

    for mat, r in ((partner, partner), (partner, yp), (partner, diag), (yp, partner), (diag, partner), (yp, diag), (diag, diag)):
        to_partner(ws.at[0], mat, r, sd.at[0]).wait_recv()
    for c in send_x + own_sends:
        c.wait_send()
    for c in local_b:
        c.wait()


def tail(x5, wg, weight, lr, decay, out_scale):
    mats, rows, cols = weight.shape
    all_rows = DP * rows
    dma = pltpu.SemaphoreType.DMA
    hbm = pl.BlockSpec(memory_space=pl.ANY)
    smem = pl.BlockSpec(memory_space=pltpu.SMEM)
    b16 = pltpu.VMEM((DP, rows, cols), BF16)
    f32 = pltpu.VMEM((DP, rows, cols), F32)
    return pl.pallas_call(
        functools.partial(tail_kernel, out_scale),
        out_shape=(jax.ShapeDtypeStruct(weight.shape, F32), jax.ShapeDtypeStruct((mats, all_rows, cols), BF16)),
        in_specs=[hbm] * 5 + [smem] * 2,
        out_specs=[hbm] * 2,
        scratch_shapes=[b16, pltpu.VMEM((DP - 1, rows, cols), F32), f32, b16, b16, b16, f32,
                        dma((DP,)), dma((DP - 1,)), dma((DP,)), dma((DP,)), dma((DP,)), dma((DP,)), dma((2,)), dma((DP,)),
                        dma((DP, DP)), dma((DP,)), dma((DP,)), dma((2 * DP,)), dma((DP,))],
        compiler_params=pltpu.CompilerParams(collective_id=1, has_side_effects=True, vmem_limit_bytes=60 * 2**20),
        name="tail",
    )(x5, *wg, weight, lr, decay)


def solution(mesh):
    def local_step(grad, mom, weight, learn_rate, decay_rate):
        mom_new, ub = front(grad, mom)
        weight_late, ub = lax.optimization_barrier((weight, ub))
        me = lax.axis_index("dp")
        y, c = me // 2, me % 2
        pairs = (
            (2 * y + (1 - c), [(0, 1), (1, 0), (2, 3), (3, 2)]),
            (2 * (1 - y) + c, [(0, 2), (2, 0), (1, 3), (3, 1)]),
            (2 * (1 - y) + (1 - c), [(0, 3), (3, 0), (1, 2), (2, 1)]),
        )
        wg = [lax.ppermute(lax.dynamic_index_in_dim(weight_late, peer, 0, keepdims=False), "dp", perm)
              for peer, perm in pairs]
        x5 = ortho(ub)
        out_scale = 0.2 * math.sqrt(max(grad.shape[2], grad.shape[3] * TP))
        weight_new, weight_full = tail(x5, wg, weight, learn_rate, decay_rate.reshape(1), out_scale)
        return mom_new, weight_new, weight_full

    return jax.shard_map(
        local_step,
        mesh=mesh,
        in_specs=(P(("rep", "dp"), None, None, "tp"), P("rep", "dp", "tp"), P("rep", "dp", "tp"), P("rep"), P()),
        out_specs=(P("rep", "dp", "tp"), P("rep", "dp", "tp"), P("rep", None, "tp")),
        check_vma=False,
    )
```

time: 653 us -> 341 us (0.52); the launches traced: 643 us -> 341 us
  waiting for transfers between devices: 361 us -> 0.01 us
  Pallas kernels: 0 us -> 274 us
  matrix products: 168 us -> 0 us
  other arithmetic: 43.9 us -> 0 us
  starting transfers between devices: 3.73 us -> 45.5 us
  blocking collectives: 28.8 us -> 0 us
  between operations: 15.6 us -> 1.41 us
    pallas_call x0 -> x3, Pallas kernels: none -> 274 us  [the longest x1 135 us: front(): pl.pallas_call(front_kernel, out_shape=(jax.ShapeDtypeStruct(mom.shape, F...]
    all_gather x2 -> x0, waiting for transfers between devices: 206 us -> none  [the longest x1 150 us: local_step(): whole_mats = lax.all_gather(whole_rows, 'tp', axis=2, tiled=True)]
    dot_general x10 -> x0, matrix products: 168 us -> none  [the longest x5 94.6 us: newton_schulz(): jnp.einsum('bij,bjk->bik', poly_mat, x_cur, preferred_element_type=jnp.fl...]
    reduce_scatter x1 -> x0, waiting for transfers between devices: 130 us -> none  [local_step(): lax.psum_scatter(grad_local[0], 'dp', scatter_dimension=1, tiled=True)]
    ppermute x0 -> x3, starting transfers between devices: none -> 45.5 us  [local_step(): lax.ppermute(lax.dynamic_index_in_dim(weight_late, peer, 0, keepdims=Fals...]
    all_to_all x1 -> x0, blocking collectives: 28.8 us -> none  [local_step(): lax.all_to_all(update, 'dp', split_axis=0, concat_axis=1, tiled=True)]
    all_to_all x1 -> x0, waiting for transfers between devices: 24.7 us -> none  [local_step(): lax.all_to_all(own_cols, 'dp', split_axis=1, concat_axis=0, tiled=True)]
    convert_element_type x3 -> x0, other arithmetic: 14.9 us -> none  [the longest x1 7.11 us: local_step(): update = (grad_mean + MOMENTUM * mom_new).astype(jnp.bfloat16)]
  transfers between devices with their start and end apart: 4 -> 3, of which waited for: 4 -> 0; matrix products, arithmetic and copies ran while one was open for 0% -> 0% of each run, Pallas kernels for 0% -> 26%
where the time goes in v1:
time: 341 us
  Pallas kernels  274 us (80%)
  starting transfers between devices  45.5 us (13%)
  local copies, waits for them, and re-layouts  20 us (6%)
    pallas_call x1, Pallas kernels, front(): pl.pallas_call(front_kernel, out_shape=(jax.ShapeDtypeStruct(mom.shape, F...  135 us
    pallas_call x1, Pallas kernels, ortho(): pl.pallas_call(ortho_kernel, out_shape=jax.ShapeDtypeStruct((size, part),...  87.7 us
    pallas_call x1, Pallas kernels, tail(): pl.pallas_call(functools.partial(tail_kernel, out_scale), out_shape=(jax....  50.5 us
    ppermute x3, starting transfers between devices, local_step(): lax.ppermute(lax.dynamic_index_in_dim(weight_late, peer, 0, keepdims=Fals...  45.5 us
    unnamed x11, local copies, waits for them, and re-layouts  16.3 us
  transfers between devices with their start and end apart: 3, of which 0 were waited for; matrix products, arithmetic and copies ran while one was open for 0% of the time, Pallas kernels for 26%

profile of v1, /device:TPU:0, one launch (start us, length us, event | category | flops | bytes accessed | tf_op | source)
XLA Modules:
  0.0 340.6 jit_solution(10827314834633610084)
XLA Ops:
  0.7 135.4 %front.1 = (f32[4,256,1024]{2,1,0:T(8,128)}, bf16[4,1024,1024]{2,1,0:T(8,128)(2,1)}) custom-call(f32[1,4,1024,1024]{3,2,1,0:T(8,128)} %grad.1, f32[4,256,1024]{2,1,0:T(8,128)} %mom.1), custom_call_target="tpu_custom_call" | custom-call | tf_op jit(solution)/shard_map/front/pallas_call | solution.py:255
  136.1 3.7 %dynamic-slice_bitcast_fusion = (f32[256,1024]{1,0:T(8,128)}, f32[256,1024]{1,0:T(8,128)}, f32[256,1024]{1,0:T(8,128)}) fusion(f32[4,256,1024]{2,1,0:T(8,128)} %weight.1, s32[]{:T(128)S(6)} %select_n.25, s32[]{:T(128)S(6)} %select_n.24, s32[]{:T(128)S(6)} %select_n.23), kind=kLoop, calls=%fused_computation | loop fusion | bytes 6291468 | tf_op jit(solution)/shard_map/jit(dynamic_index_in_dim)/squeeze | solution.py:469
  139.8 44.5 %collective-permute-start.2 = (f32[256,1024]{1,0:T(8,128)}, f32[256,1024]{1,0:T(8,128)S(1)}, u32[]{:S(2)}, u32[]{:S(2)}) collective-permute-start(f32[256,1024]{1,0:T(8,128)} %get-tuple-element.15), channel_id=1, source_target_pairs={{0,3},{3,0},{1,2},{2,1},{4,7},{7,4},{5,6},{6,5},{8,11},{11,8},{9,1... | collective-permute-start | bytes 3145736 | tf_op jit(solution)/shard_map/ppermute | solution.py:469
  184.3 1.0 collective-permute-start.1
  185.3 0.0 collective-permute-start
  185.3 87.7 %ortho.1.x5 = bf16[1024,1024]{1,0:T(8,128)(2,1)} custom-call(bf16[4,1024,1024]{2,1,0:T(8,128)(2,1)} %get-tuple-element.11.u), custom_call_target="tpu_custom_call" | custom-call | flops 96636764160 | bytes 8388608 | tf_op jit(solution)/shard_map/ortho/pallas_call | solution.py:322
  273.7 0.0 collective-permute-done.2.wg_diag
  273.7 0.0 copy-start.1
  273.7 0.0 collective-permute-done.1.wg_yp
  273.7 0.0 copy-start.2
  273.7 0.0 collective-permute-done.wg_p
  273.7 0.0 copy-start.3
  273.7 0.9 copy-done.1
  274.6 0.3 copy-done.2
  275.0 0.3 copy-done.3
  275.3 50.5 %tail.1 = (f32[4,256,1024]{2,1,0:T(8,128)}, bf16[4,1024,1024]{2,1,0:T(8,128)(2,1)}) custom-call(bf16[1024,1024]{1,0:T(8,128)(2,1)} %ortho.1.x5, f32[256,1024]{1,0:T(8,128)} %copy-done.3, f32[256,1024]{1,0:T(8,128)} %copy-done.2, f32[256,1024]{1,0:T(8,128)} %copy-done.1, f32[4,256,1024]{2,1,0:T(8,128)} %weight.1, f32[4]{0:T(128)} %lr.1, f32[1]{0:T(128)} %bitcast.7.decay), custom_call_target="tpu_custom_call" | custom-call | tf_op jit(solution)/shard_map/tail/pallas_call | solution.py:445
  325.8 0.0 copy-start
  325.9 4.9 %copy.12 = f32[4,256,1024]{2,1,0:T(8,128)} copy(f32[4,256,1024]{2,1,0:T(8,128)} %get-tuple-element.21) | data formatting | bytes 8388608
  330.8 0.0 copy-done
  330.8 2.0 copy.13
  332.8 7.8 %copy.14 = bf16[4,1024,1024]{2,1,0:T(8,128)(2,1)} copy(bf16[4,1024,1024]{2,1,0:T(8,128)(2,1)} %get-tuple-element.23) | data formatting | bytes 16777216
Async XLA Ops:
  139.8 133.8 %collective-permute-start.2 = (f32[256,1024]{1,0:T(8,128)}, f32[256,1024]{1,0:T(8,128)S(1)}, u32[]{:S(2)}, u32[]{:S(2)}) collective-permute-start(f32[256,1024]{1,0:T(8,128)} %get-tuple-element.15), channel_id=1, source_target_pairs={{0,3},{3,0},{1,2},{2,1},{4,7},{7,4},{5,6},{6,5},{8,11},{11,8},{9,1... | collective-permute-start | bytes 3145736 | tf_op jit(solution)/shard_map/ppermute | solution.py:469
  184.3 89.3 %collective-permute-start.1 = (f32[256,1024]{1,0:T(8,128)}, f32[256,1024]{1,0:T(8,128)S(1)}, u32[]{:S(2)}, u32[]{:S(2)}) collective-permute-start(f32[256,1024]{1,0:T(8,128)} %get-tuple-element.16), channel_id=1, source_target_pairs={{0,2},{2,0},{1,3},{3,1},{4,6},{6,4},{5,7},{7,5},{8,10},{10,8},{9,1... | collective-permute-start | bytes 3145736 | tf_op jit(solution)/shard_map/ppermute | solution.py:469
  185.3 88.4 %collective-permute-start = (f32[256,1024]{1,0:T(8,128)}, f32[256,1024]{1,0:T(8,128)S(1)}, u32[]{:S(2)}, u32[]{:S(2)}) collective-permute-start(f32[256,1024]{1,0:T(8,128)} %get-tuple-element.17), channel_id=1, source_target_pairs={{0,1},{1,0},{2,3},{3,2},{4,5},{5,4},{6,7},{7,6},{8,9},{9,8},{10,11... | collective-permute-start | bytes 3145736 | tf_op jit(solution)/shard_map/ppermute | solution.py:469
  273.7 1.0 copy-start.1
  273.7 1.3 copy-start.2
  273.7 1.6 copy-start.3
  325.8 5.0 %copy-start = (f32[4,256,1024]{2,1,0:T(8,128)S(1)}, f32[4,256,1024]{2,1,0:T(8,128)}, u32[]{:S(2)}) copy-start(f32[4,256,1024]{2,1,0:T(8,128)} %get-tuple-element.22) | copy-start | bytes 12582916

commit v2 on v0

v2 whole, which is shorter than its diff:
```python
import functools
import math

import jax
import jax.numpy as jnp
from jax import lax
from jax.experimental import pallas as pl
from jax.experimental.pallas import tpu as pltpu
from jax.sharding import PartitionSpec as P

MOMENTUM = 0.95
NS_STEPS = 5
COEF_A = 3.4445
COEF_B = -4.7750
COEF_C = 2.0315
NORM_EPS = 1e-7

DP = 4
TP = 4
F32 = jnp.float32
BF16 = jnp.bfloat16
NT = (((1,), (1,)), ((), ()))

ORDER = [(0, 0), (2, 0), (0, 1), (2, 1), (1, 0), (3, 0), (1, 1), (3, 1), (1, 2), (3, 2)]
PARTS = {0: [(0, 32), (32, 32)], 1: [(0, 32), (32, 16), (48, 16)]}
MAX_PARTS = 3
STAGES = {
    0: {1: (0, 1), 2: (2, 3), 3: (4, 5), 4: (6, 7), 5: (8,)},
    1: {5: (0, 1), 6: (2, 3), 7: (4, 5), 8: (6, 7), 9: (8, 9, 10, 11, 12)},
}
STEP = 32


def mesh_copy(src, dst, send, recv, **axes):
    return pltpu.make_async_remote_copy(
        src_ref=src, dst_ref=dst, send_sem=send, recv_sem=recv,
        device_id=axes, device_id_type=pl.DeviceIdType.MESH)


def dot(a, b):
    return jnp.dot(a, b, preferred_element_type=F32)


def muon_kernel(out_scale, grad, mom, weight, lr, decay,
                mom_new, w_new, wb,
                own_yp, own_me, recv_a, recv_b, recv_y, momb, ub, x, gram, poly, x5, x5e, wg, xr, ws, wo,
                ld_yp, ld_me, ld_mom, sa, ra, sb, rb, sy, ry, su, sm, ru,
                zs, zf, zr, pw, rw, lw, se, re, sx, rx, sw, rwb, sd, rd, sf, sl_b, sl_n):
    me = lax.axis_index("dp")
    z = lax.axis_index("tp")
    y, c = lax.div(me, 2), lax.rem(me, 2)
    partner, yp, diag = 2 * y + (1 - c), 2 * (1 - y) + c, 2 * (1 - y) + (1 - c)
    peers = (me, partner, yp, diag)
    rows, cols = mom.shape[1], mom.shape[2]
    unit = rows // 64
    npiece = len(ORDER)
    middle = jnp.logical_and(z > 0, z < TP - 1)
    left = z < TP // 2
    nb = jnp.where(left, z + 1, z - 1)
    other = TP - 1 - z
    end = jnp.where(left, 0, TP - 1)
    far = TP - 1 - end

    barrier = pltpu.get_barrier_semaphore()
    for peer in peers[1:]:
        pl.semaphore_signal(barrier, inc=1, device_id={"dp": peer}, device_id_type=pl.DeviceIdType.MESH)

    @pl.when(z > 0)
    def _():
        pl.semaphore_signal(barrier, inc=1, device_id={"tp": z - 1}, device_id_type=pl.DeviceIdType.MESH)

    @pl.when(z < TP - 1)
    def _():
        pl.semaphore_signal(barrier, inc=1, device_id={"tp": z + 1}, device_id_type=pl.DeviceIdType.MESH)

    def span(k):
        m, p = ORDER[k]
        lo, n = PARTS[m % 2][p]
        return m, p, lo * unit, n * unit

    def grad_rows(r, k):
        m, _, lo, n = span(k)
        return grad.at[0, m, pl.ds(pl.multiple_of(r * rows + lo, 16), n), :]

    def piece(buf, k):
        m, _, lo, n = span(k)
        return buf.at[m, pl.ds(lo, n), :]

    def load_yp(k):
        return pltpu.make_async_copy(grad_rows(yp, k), piece(own_yp, k), ld_yp.at[k])

    def load_me(k):
        return pltpu.make_async_copy(grad_rows(me, k), piece(own_me, k), ld_me.at[k])

    def load_mom(k):
        return pltpu.make_async_copy(piece(mom, k), piece(momb, k), ld_mom.at[k])

    def copy_a(k):
        return mesh_copy(grad_rows(diag, k), piece(recv_a, k), sa.at[k], ra.at[k], dp=partner)

    def copy_b(k):
        return mesh_copy(grad_rows(partner, k), piece(recv_b, k), sb.at[k], rb.at[k], dp=partner)

    def copy_y(k):
        return mesh_copy(piece(own_yp, k), piece(recv_y, k), sy.at[k], ry.at[k], dp=yp)

    def store_mom(k):
        return pltpu.make_async_copy(piece(momb, k), piece(mom_new, k), sm.at[k])

    def x_block(r, lo, n, s):
        return x.at[pl.ds(pl.multiple_of(r * rows + lo, 16), n), pl.ds(pl.multiple_of(s * cols, cols), cols)]

    def copy_u(k):
        m, p, lo, n = span(k)
        return mesh_copy(piece(ub, k), x_block(me, lo, n, z), su.at[k], ru.at[me, p], dp=m)

    for k in range(npiece):
        load_yp(k).start()
    for k in range(npiece):
        load_me(k).start()
        load_mom(k).start()
    pl.semaphore_wait(barrier, 3 + jnp.where(z > 0, 1, 0) + jnp.where(z < TP - 1, 1, 0))
    for k in range(npiece):
        copy_a(k).start()
    for k in range(npiece):
        copy_b(k).start()

    def chip_sum(k):
        m, _, lo, n = span(k)
        load_yp(k).wait()
        copy_a(k).wait_recv()

        @pl.loop(0, n // STEP)
        def _(i):
            sl = pl.ds(pl.multiple_of(lo + i * STEP, STEP), STEP)
            own_yp[m, sl, :] = own_yp[m, sl, :] + recv_a[m, sl, :]

    def update_piece(k):
        m, _, lo, n = span(k)
        load_me(k).wait()
        copy_b(k).wait_recv()
        load_mom(k).wait()
        copy_y(k).wait_recv()

        @pl.loop(0, n // STEP)
        def _(i):
            sl = pl.ds(pl.multiple_of(lo + i * STEP, STEP), STEP)
            g = (own_me[m, sl, :] + recv_b[m, sl, :] + recv_y[m, sl, :]) * (1.0 / DP)
            mn = MOMENTUM * momb[m, sl, :] + g
            momb[m, sl, :] = mn
            ub[m, sl, :] = (g + MOMENTUM * mn).astype(BF16)

        @pl.when(me == m)
        def _():
            x[pl.ds(pl.multiple_of(me * rows + lo, 16), n), pl.ds(pl.multiple_of(z * cols, cols), cols)] = ub[m, lo:lo + n, :]

        @pl.when(me != m)
        def _():
            copy_u(k).start()

        store_mom(k).start()

    def gather(core):
        todo = [(p, lo * unit, n * unit, i) for p, (lo, n) in enumerate(PARTS[core]) for i in range(DP)]

        def copy_own(q):
            _, lo, n, i = todo[q]
            blk = x_block(peers[i], lo, n, z)
            return mesh_copy(blk, blk, zs.at[q], zr.at[z, q], tp=nb)

        def copy_on(q):
            _, lo, n, i = todo[q]
            blk = x_block(peers[i], lo, n, end)
            return mesh_copy(blk, blk, zf.at[q], zr.at[end, q], tp=other)

        def landed(q, s):
            _, lo, n, i = todo[q]
            blk = x_block(peers[i], lo, n, s)
            mesh_copy(blk, blk, zs.at[q], zr.at[s, q], tp=nb).wait_recv()

        def stage(t):
            if t < len(todo):
                p, lo, n, i = todo[t]
                if i > 0:
                    mesh_copy(ub.at[0, pl.ds(0, n), :], x_block(peers[i], lo, n, z), su.at[0], ru.at[peers[i], p],
                              dp=peers[i]).wait_recv()
                copy_own(t).start()
            if t > 0:
                @pl.when(middle)
                def _():
                    landed(t - 1, end)
                    copy_on(t - 1).start()

        def finish():
            for q in range(len(todo)):
                @pl.when(middle)
                def _():
                    landed(q, other)
                    landed(q, far)

        def drain():
            for q in range(len(todo)):
                copy_own(q).wait_send()

                @pl.when(middle)
                def _():
                    copy_on(q).wait_send()

        return stage, finish, drain

    gathers = [gather(0), gather(1)]

    def on_core(core, fn):
        @pl.when(c == core)
        def _():
            fn()

    chip_sum(0)
    chip_sum(1)
    copy_y(0).start()
    copy_y(1).start()
    for k in range(npiece):
        if k + 2 < npiece:
            chip_sum(k + 2)
        update_piece(k)
        if k + 2 < npiece:
            copy_y(k + 2).start()
        for core in range(2):
            if k in STAGES[core]:
                on_core(core, lambda: [gathers[core][0](t) for t in STAGES[core][k]])
    for core in range(2):
        on_core(core, gathers[core][1])
        on_core(core, gathers[core][2])

    def copy_w(i):
        return mesh_copy(weight.at[peers[i]], wg.at[i - 1], pw.at[i], rw.at[i], dp=peers[i])

    wv = own_me
    load_w = [pltpu.make_async_copy(weight.at[peers[i]], wv.at[i], lw.at[i]) for i in range(DP)]
    for i in range(1, DP):
        copy_w(i).start()
    for cp in load_w:
        cp.start()

    size, width = x.shape
    block = 256
    nblk = size // block

    def column(s):
        return pl.ds(pl.multiple_of(s * cols, cols), cols)

    def row_block(r):
        return pl.ds(pl.multiple_of(r * rows, rows), rows)

    def make_poly():
        for i in range(nblk):
            for j in range(i, nblk):
                blk = lax.dot_general(x[i * block:(i + 1) * block, :], x[j * block:(j + 1) * block, :], NT,
                                      preferred_element_type=F32).astype(BF16)
                gram[i * block:(i + 1) * block, j * block:(j + 1) * block] = blk
                if j > i:
                    gram[j * block:(j + 1) * block, i * block:(i + 1) * block] = blk.T
        poly[...] = (COEF_B * gram[...].astype(F32) + COEF_C * dot(gram[...], gram[...])).astype(BF16)

    @pl.when(middle)
    def _():
        def square_sum(i, acc):
            v = x[pl.ds(pl.multiple_of(i * 16, 16), 16), :].astype(F32)
            return acc + v * v

        total = lax.fori_loop(0, size // 16, square_sum, jnp.zeros((16, width), F32))
        inv = 1.0 / (jnp.sqrt(jnp.sum(total, keepdims=True)) + NORM_EPS)

        @pl.loop(0, size // 16)
        def _(i):
            sl = pl.ds(pl.multiple_of(i * 16, 16), 16)
            x[sl, :] = (x[sl, :].astype(F32) * inv).astype(BF16)

        @pl.loop(0, NS_STEPS)
        def _(step):
            make_poly()

            @pl.when(step < NS_STEPS - 1)
            def _():
                @pl.loop(0, TP)
                def _(t):
                    cs = column(t)
                    xc = x[:, cs]
                    x[:, cs] = (COEF_A * xc.astype(F32) + dot(poly[...], xc)).astype(BF16)

    def copy_e(i):
        blk = row_block(peers[i])
        return mesh_copy(x5e.at[blk, :], x5.at[blk, :], se.at[i], re.at[i], tp=end)

    def last(i, s, dst):
        blk = row_block(peers[i])
        dst[blk, :] = (COEF_A * x[blk, column(s)].astype(F32) + dot(poly[blk, :], x[:, column(s)])).astype(BF16)

    def apply(w, v, mat):
        return w - lr[mat] * (out_scale * v.astype(F32) + decay[0] * w)

    def each(fn):
        @pl.loop(0, rows // STEP)
        def _(i):
            fn(pl.ds(pl.multiple_of(i * STEP, STEP), STEP))

    def to_partner(src, mat, r, sem):
        return mesh_copy(src, wb.at[mat, row_block(r), :], sem, rd.at[mat, r], dp=partner)

    sends = []
    stores = []

    def go(cp, into):
        cp.start()
        into.append(cp)

    for i in (2, 3, 0, 1):
        r = peers[i]

        @pl.when(middle)
        def _():
            last(i, end, x5e)
            copy_e(i).start()
            last(i, z, x5)

        @pl.when(jnp.logical_not(middle))
        def _():
            copy_e(i).wait_recv()

        if i > 0:
            go(mesh_copy(x5.at[row_block(r), :], xr.at[me], sx.at[i], rx.at[me], dp=r), sends)
        if i == 0:
            load_w[0].wait()

            def own(sl):
                w = apply(wv[0, sl, :], x5[pl.ds(me * rows + sl.start, STEP), :], me)
                wv[0, sl, :] = w
                ws[0, sl, :] = w.astype(BF16)
            each(own)
            go(pltpu.make_async_copy(wv.at[0], w_new.at[me], sl_n.at[0]), stores)
        else:
            copy_w(i).wait_recv()

            def rest(sl, i=i, r=r):
                ws[i, sl, :] = apply(wg[i - 1, sl, :], x5[pl.ds(r * rows + sl.start, STEP), :], me).astype(BF16)
            each(rest)
        if i < 2:
            go(mesh_copy(ws.at[i], wb.at[me, row_block(r), :], sw.at[i], rwb.at[me], dp=peers[2 + i]), sends)
        if i != 1:
            go(to_partner(ws.at[i], me, r, sd.at[i]), sends)
        go(pltpu.make_async_copy(ws.at[i], wb.at[me, row_block(r), :], sl_b.at[i]), stores)

    for i in range(1, DP):
        mat = peers[i]
        load_w[i].wait()
        mesh_copy(x5.at[row_block(me), :], xr.at[mat], sx.at[0], rx.at[mat], dp=mat).wait_recv()

        def mine(sl, i=i, mat=mat):
            w = apply(wv[i, sl, :], xr[mat, sl, :], mat)
            wv[i, sl, :] = w
            wo[i, sl, :] = w.astype(BF16)
        each(mine)
        if i > 1:
            go(to_partner(wo.at[i], mat, me, sf.at[i]), sends)
        go(pltpu.make_async_copy(wv.at[i], w_new.at[mat], sl_n.at[i]), stores)
        go(pltpu.make_async_copy(wo.at[i], wb.at[mat, row_block(me), :], sl_b.at[DP + i]), stores)

    for i in (2, 3):
        dst = wb.at[peers[i], row_block(yp), :]
        mesh_copy(ws.at[0], dst, sw.at[0], rwb.at[peers[i]], dp=peers[i]).wait_recv()
        go(to_partner(dst, peers[i], yp, sf.at[DP + i]), sends)

    for mat, r in ((partner, partner), (partner, yp), (partner, diag), (yp, partner), (diag, partner), (yp, diag), (diag, diag)):
        to_partner(ws.at[0], mat, r, sd.at[0]).wait_recv()

    for k in range(npiece):
        copy_a(k).wait_send()
        copy_b(k).wait_send()
        copy_y(k).wait_send()
        store_mom(k).wait()

        @pl.when(me != ORDER[k][0])
        def _():
            copy_u(k).wait_send()
    for i in range(DP):
        if i > 0:
            copy_w(i).wait_send()

        @pl.when(middle)
        def _():
            copy_e(i).wait_send()
    for cp in sends:
        cp.wait_send()
    for cp in stores:
        cp.wait()


def muon(grad, mom, weight, lr, decay, out_scale):
    _, mats, all_rows, cols = grad.shape
    rows = mom.shape[1]
    n = len(ORDER)
    nq = DP * MAX_PARTS
    dma = pltpu.SemaphoreType.DMA
    hbm = pl.BlockSpec(memory_space=pl.ANY)
    smem = pl.BlockSpec(memory_space=pltpu.SMEM)
    f32 = pltpu.VMEM((mats, rows, cols), F32)
    b16 = pltpu.VMEM((mats, rows, cols), BF16)
    square = pltpu.VMEM((all_rows, all_rows), BF16)
    slab = pltpu.VMEM((all_rows, cols), BF16)
    return pl.pallas_call(
        functools.partial(muon_kernel, out_scale),
        out_shape=(jax.ShapeDtypeStruct(mom.shape, F32), jax.ShapeDtypeStruct(weight.shape, F32),
                   jax.ShapeDtypeStruct((mats, all_rows, cols), BF16)),
        in_specs=[hbm] * 3 + [smem] * 2,
        out_specs=[hbm] * 3,
        scratch_shapes=[f32] * 6 + [b16, pltpu.VMEM((all_rows, TP * cols), BF16), square, square, slab, slab,
                                    pltpu.VMEM((DP - 1, rows, cols), F32), b16, b16, b16]
        + [dma((n,))] * 11 + [dma((DP, MAX_PARTS)), dma((nq,)), dma((nq,)), dma((TP, nq))]
        + [dma((DP,))] * 9 + [dma((DP,)), dma((DP, DP)), dma((2 * DP,)), dma((2 * DP,)), dma((DP,))],
        compiler_params=pltpu.CompilerParams(collective_id=0, has_side_effects=True, vmem_limit_bytes=67043328),
        name="muon",
    )(grad, mom, weight, lr, decay)


def solution(mesh):
    def local_step(grad, mom, weight, learn_rate, decay_rate):
        out_scale = 0.2 * math.sqrt(max(grad.shape[2], grad.shape[3] * TP))
        return muon(grad, mom, weight, learn_rate, decay_rate.reshape(1), out_scale)

    return jax.shard_map(
        local_step,
        mesh=mesh,
        in_specs=(P(("rep", "dp"), None, None, "tp"), P("rep", "dp", "tp"), P("rep", "dp", "tp"), P("rep"), P()),
        out_specs=(P("rep", "dp", "tp"), P("rep", "dp", "tp"), P("rep", None, "tp")),
        check_vma=False,
    )
```

time: 653 us -> 281 us (0.43); the launches traced: 643 us -> 281 us
  waiting for transfers between devices: 361 us -> 0 us
  Pallas kernels: 0 us -> 265 us
  matrix products: 168 us -> 0 us
  other arithmetic: 43.9 us -> 0 us
  blocking collectives: 28.8 us -> 0 us
  between operations: 15.6 us -> 1.3 us
  local copies, waits for them, and re-layouts: 22 us -> 14.7 us
    pallas_call x0 -> x1, Pallas kernels: none -> 265 us  [muon(): pl.pallas_call(functools.partial(muon_kernel, out_scale), out_shape=(jax....]
    all_gather x2 -> x0, waiting for transfers between devices: 206 us -> none  [the longest x1 150 us: local_step(): whole_mats = lax.all_gather(whole_rows, 'tp', axis=2, tiled=True)]
    dot_general x10 -> x0, matrix products: 168 us -> none  [the longest x5 94.6 us: newton_schulz(): jnp.einsum('bij,bjk->bik', poly_mat, x_cur, preferred_element_type=jnp.fl...]
    reduce_scatter x1 -> x0, waiting for transfers between devices: 130 us -> none  [local_step(): lax.psum_scatter(grad_local[0], 'dp', scatter_dimension=1, tiled=True)]
    all_to_all x1 -> x0, blocking collectives: 28.8 us -> none  [local_step(): lax.all_to_all(update, 'dp', split_axis=0, concat_axis=1, tiled=True)]
    all_to_all x1 -> x0, waiting for transfers between devices: 24.7 us -> none  [local_step(): lax.all_to_all(own_cols, 'dp', split_axis=1, concat_axis=0, tiled=True)]
    convert_element_type x3 -> x0, other arithmetic: 14.9 us -> none  [the longest x1 7.11 us: local_step(): update = (grad_mean + MOMENTUM * mom_new).astype(jnp.bfloat16)]
    unnamed x1 -> x0, other arithmetic: 12.8 us -> none
  transfers between devices with their start and end apart: 4 -> 0, of which waited for: 4 -> 0; matrix products, arithmetic and copies ran while one was open for 0% -> 0% of each run, Pallas kernels for 0% -> 0%
where the time goes in v2:
time: 281 us
  Pallas kernels  265 us (94%)
  local copies, waits for them, and re-layouts  14.7 us (5%)
    pallas_call x1, Pallas kernels, muon(): pl.pallas_call(functools.partial(muon_kernel, out_scale), out_shape=(jax....  265 us
    unnamed x5, local copies, waits for them, and re-layouts  14.7 us

profile of v2, /device:TPU:0, one launch (start us, length us, event | category | flops | bytes accessed | tf_op | source)
XLA Modules:
  0.0 280.6 jit_solution(830244861288847808)
XLA Ops:
  1.3 264.6 %muon.1 = (f32[4,256,1024]{2,1,0:T(8,128)}, f32[4,256,1024]{2,1,0:T(8,128)}, bf16[4,1024,1024]{2,1,0:T(8,128)(2,1)}) custom-call(f32[1,4,1024,1024]{3,2,1,0:T(8,128)} %grad.1, f32[4,256,1024]{2,1,0:T(8,128)} %mom.1, f32[4,256,1024]{2,1,0:T(8,128)} %weight.1, f32[4]{0:T(128)} %lr.1, f32[1]{0:T(128)} %bitcast.1.decay), custom_call_target="tpu_custom_call" | custom-call | tf_op jit(solution)/shard_map/muon/pallas_call | solution.py:410
  265.9 0.0 copy-start
  265.9 4.9 %copy.12 = f32[4,256,1024]{2,1,0:T(8,128)} copy(f32[4,256,1024]{2,1,0:T(8,128)} %get-tuple-element.6) | data formatting | bytes 8388608
  270.8 0.0 copy-done
  270.8 2.0 copy.13
  272.8 7.8 %copy.14 = bf16[4,1024,1024]{2,1,0:T(8,128)(2,1)} copy(bf16[4,1024,1024]{2,1,0:T(8,128)(2,1)} %get-tuple-element.8) | data formatting | bytes 16777216
Async XLA Ops:
  265.9 5.0 %copy-start = (f32[4,256,1024]{2,1,0:T(8,128)S(1)}, f32[4,256,1024]{2,1,0:T(8,128)}, u32[]{:S(2)}) copy-start(f32[4,256,1024]{2,1,0:T(8,128)} %get-tuple-element.7) | copy-start | bytes 12582916

commit v3 on v2

--- a/solution.py
+++ b/solution.py
@@ -21,13 +21,17 @@
 BF16 = jnp.bfloat16
 NT = (((1,), (1,)), ((), ()))
 
-ORDER = [(0, 0), (2, 0), (0, 1), (2, 1), (1, 0), (3, 0), (1, 1), (3, 1), (1, 2), (3, 2)]
-PARTS = {0: [(0, 32), (32, 32)], 1: [(0, 32), (32, 16), (48, 16)]}
-MAX_PARTS = 3
+ORDER = [(0, 0), (2, 0), (0, 1), (2, 1), (1, 0), (3, 0), (1, 1), (3, 1), (1, 2), (3, 2), (1, 3), (3, 3)]
+PARTS = {0: [(0, 32), (32, 32)], 1: [(0, 32), (32, 16), (48, 8), (56, 8)]}
+MAX_PARTS = 4
+SENT = [3, 4, 5, 6, 7, 8, 9, 10, 12, 12, 12, 12]
 STAGES = {
-    0: {1: (0, 1), 2: (2, 3), 3: (4, 5), 4: (6, 7), 5: (8,)},
-    1: {5: (0, 1), 6: (2, 3), 7: (4, 5), 8: (6, 7), 9: (8, 9, 10, 11, 12)},
+    (0, 0): {0: (0, 1), 1: (2, 3), 2: (4, 5), 3: (6, 7), 4: (8,)},
+    (0, 1): {1: (0, 1), 2: (2, 3), 3: (4, 5), 4: (6, 7), 5: (8,)},
+    (1, 0): {4: (0, 1), 5: (2, 3), 6: (4, 5), 7: (6, 7), 8: (8, 9), 9: (10, 11), 10: (12, 13), 11: (14, 15, 16)},
+    (1, 1): {5: (0, 1), 6: (2, 3), 7: (4, 5), 8: (6, 7), 9: (8, 9), 10: (10, 11), 11: (12, 13, 14, 15, 16)},
 }
+HEAD = 5
 STEP = 32
 
 
@@ -43,7 +47,7 @@
 
 def muon_kernel(out_scale, grad, mom, weight, lr, decay,
                 mom_new, w_new, wb,
-                own_yp, own_me, recv_a, recv_b, recv_y, momb, ub, x, gram, poly, x5, x5e, wg, xr, ws, wo,
+                own_yp, own_me, recv_a, recv_b, recv_y, momb, ub, x, gram, poly, x5, x5e, wg, xr, ws, wo, ssq,
                 ld_yp, ld_me, ld_mom, sa, ra, sb, rb, sy, ry, su, sm, ru,
                 zs, zf, zr, pw, rw, lw, se, re, sx, rx, sw, rwb, sd, rd, sf, sl_b, sl_n):
     me = lax.axis_index("dp")
@@ -197,6 +201,15 @@
                 def _():
                     landed(q, other)
                     landed(q, far)
+                    _, lo, n, i = todo[q]
+                    base = peers[i] * rows + lo
+
+                    def square_sum(t, acc):
+                        v = x[pl.ds(pl.multiple_of(base + t * 16, 16), 16), :].astype(F32)
+                        return acc + v * v
+
+                    part = lax.fori_loop(0, n // 16, square_sum, jnp.zeros(ssq.shape, F32))
+                    ssq[...] = part if q == 0 else ssq[...] + part
 
         def drain():
             for q in range(len(todo)):
@@ -215,33 +228,6 @@
         def _():
             fn()
 
-    chip_sum(0)
-    chip_sum(1)
-    copy_y(0).start()
-    copy_y(1).start()
-    for k in range(npiece):
-        if k + 2 < npiece:
-            chip_sum(k + 2)
-        update_piece(k)
-        if k + 2 < npiece:
-            copy_y(k + 2).start()
-        for core in range(2):
-            if k in STAGES[core]:
-                on_core(core, lambda: [gathers[core][0](t) for t in STAGES[core][k]])
-    for core in range(2):
-        on_core(core, gathers[core][1])
-        on_core(core, gathers[core][2])
-
-    def copy_w(i):
-        return mesh_copy(weight.at[peers[i]], wg.at[i - 1], pw.at[i], rw.at[i], dp=peers[i])
-
-    wv = own_me
-    load_w = [pltpu.make_async_copy(weight.at[peers[i]], wv.at[i], lw.at[i]) for i in range(DP)]
-    for i in range(1, DP):
-        copy_w(i).start()
-    for cp in load_w:
-        cp.start()
-
     size, width = x.shape
     block = 256
     nblk = size // block
@@ -252,7 +238,15 @@
     def row_block(r):
         return pl.ds(pl.multiple_of(r * rows, rows), rows)
 
-    def make_poly():
+    def normalize():
+        inv = 1.0 / (jnp.sqrt(jnp.sum(ssq[...], keepdims=True)) + NORM_EPS)
+
+        @pl.loop(0, size // 16)
+        def _(i):
+            sl = pl.ds(pl.multiple_of(i * 16, 16), 16)
+            x[sl, :] = (x[sl, :].astype(F32) * inv).astype(BF16)
+
+    def square():
         for i in range(nblk):
             for j in range(i, nblk):
                 blk = lax.dot_general(x[i * block:(i + 1) * block, :], x[j * block:(j + 1) * block, :], NT,
@@ -260,33 +254,93 @@
                 gram[i * block:(i + 1) * block, j * block:(j + 1) * block] = blk
                 if j > i:
                     gram[j * block:(j + 1) * block, i * block:(i + 1) * block] = blk.T
-        poly[...] = (COEF_B * gram[...].astype(F32) + COEF_C * dot(gram[...], gram[...])).astype(BF16)
+
+    def polynomial():
+        for i in range(nblk):
+            ra, rb = i * block, (i + 1) * block
+            strip = (COEF_B * gram[ra:rb, ra:].astype(F32) + COEF_C * dot(gram[ra:rb, :], gram[:, ra:])).astype(BF16)
+            poly[ra:rb, ra:] = strip
+            for j in range(i + 1, nblk):
+                poly[j * block:(j + 1) * block, ra:rb] = strip[:, j * block - ra:(j + 1) * block - ra].T
+
+    def update(lo, hi):
+        @pl.loop(lo, hi)
+        def _(t):
+            cs = column(t)
+            xc = x[:, cs]
+            x[:, cs] = (COEF_A * xc.astype(F32) + dot(poly[...], xc)).astype(BF16)
+
+    def in_middle(fn):
+        @pl.when(middle)
+        def _():
+            fn()
+
+    def head(k):
+        if k == HEAD:
+            gathers[0][1]()
+            gathers[0][2]()
+
+            def begin():
+                normalize()
+                square()
+            in_middle(begin)
+        if k == HEAD + 1:
+            in_middle(polynomial)
+        if k == HEAD + 2:
+            in_middle(lambda: update(0, TP // 2))
+        if k == npiece - 1:
+            in_middle(lambda: update(TP // 2, TP))
+
+    chip_sum(0)
+    chip_sum(1)
+    copy_y(0).start()
+    copy_y(1).start()
+    sent = 2
+    for k in range(npiece):
+        for j in range(sent, SENT[k]):
+            chip_sum(j)
+        update_piece(k)
+        for j in range(sent, SENT[k]):
+            copy_y(j).start()
+        sent = SENT[k]
+        for (core, chip), stages in STAGES.items():
+            if k in stages:
+                @pl.when(jnp.logical_and(c == core, y == chip))
+                def _():
+                    for t in stages[k]:
+                        gathers[core][0](t)
+        if k in (HEAD, HEAD + 1, HEAD + 2):
+            on_core(0, lambda: head(k))
+
+    def copy_w(i):
+        return mesh_copy(weight.at[peers[i]], wg.at[i - 1], pw.at[i], rw.at[i], dp=peers[i])
+
+    wv = own_me
+    load_w = [pltpu.make_async_copy(weight.at[peers[i]], wv.at[i], lw.at[i]) for i in range(DP)]
+    for i in range(1, DP):
+        copy_w(i).start()
+    for cp in load_w:
+        cp.start()
+
+    on_core(0, lambda: head(npiece - 1))
+
+    def catch_up():
+        gathers[1][1]()
+        gathers[1][2]()
+        in_middle(normalize)
+    on_core(1, catch_up)
 
     @pl.when(middle)
     def _():
-        def square_sum(i, acc):
-            v = x[pl.ds(pl.multiple_of(i * 16, 16), 16), :].astype(F32)
-            return acc + v * v
-
-        total = lax.fori_loop(0, size // 16, square_sum, jnp.zeros((16, width), F32))
-        inv = 1.0 / (jnp.sqrt(jnp.sum(total, keepdims=True)) + NORM_EPS)
-
-        @pl.loop(0, size // 16)
-        def _(i):
-            sl = pl.ds(pl.multiple_of(i * 16, 16), 16)
-            x[sl, :] = (x[sl, :].astype(F32) * inv).astype(BF16)
-
-        @pl.loop(0, NS_STEPS)
-        def _(step):
-            make_poly()
-
-            @pl.when(step < NS_STEPS - 1)
+        def step(i, carry):
+            square()
+            polynomial()
+
+            @pl.when(i < NS_STEPS - 1)
             def _():
-                @pl.loop(0, TP)
-                def _(t):
-                    cs = column(t)
-                    xc = x[:, cs]
-                    x[:, cs] = (COEF_A * xc.astype(F32) + dot(poly[...], xc)).astype(BF16)
+                update(0, TP)
+            return carry
+        lax.fori_loop(1 - c, NS_STEPS, step, 0)
 
     def copy_e(i):
         blk = row_block(peers[i])
@@ -414,7 +468,7 @@
         in_specs=[hbm] * 3 + [smem] * 2,
         out_specs=[hbm] * 3,
         scratch_shapes=[f32] * 6 + [b16, pltpu.VMEM((all_rows, TP * cols), BF16), square, square, slab, slab,
-                                    pltpu.VMEM((DP - 1, rows, cols), F32), b16, b16, b16]
+                                    pltpu.VMEM((DP - 1, rows, cols), F32), b16, b16, b16, pltpu.VMEM((16, TP * cols), F32)]
         + [dma((n,))] * 11 + [dma((DP, MAX_PARTS)), dma((nq,)), dma((nq,)), dma((TP, nq))]
         + [dma((DP,))] * 9 + [dma((DP,)), dma((DP, DP)), dma((2 * DP,)), dma((2 * DP,)), dma((DP,))],
         compiler_params=pltpu.CompilerParams(collective_id=0, has_side_effects=True, vmem_limit_bytes=67043328),

time: 281 us -> 267 us (0.950)
  Pallas kernels: 265 us -> 251 us
    pallas_call x1, Pallas kernels: 265 us -> 251 us  [muon(): pl.pallas_call(functools.partial(muon_kernel, out_scale), out_shape=(jax....]
where the time goes in v3:
time: 267 us
  Pallas kernels  251 us (94%)
  local copies, waits for them, and re-layouts  14.7 us (6%)
    pallas_call x1, Pallas kernels, muon(): pl.pallas_call(functools.partial(muon_kernel, out_scale), out_shape=(jax....  251 us
    unnamed x5, local copies, waits for them, and re-layouts  14.7 us

profile of v3, /device:TPU:0, one launch (start us, length us, event | category | flops | bytes accessed | tf_op | source)
XLA Modules:
  0.0 267.3 jit_solution(9782518115324271806)
XLA Ops:
  1.3 251.3 %muon.1 = (f32[4,256,1024]{2,1,0:T(8,128)}, f32[4,256,1024]{2,1,0:T(8,128)}, bf16[4,1024,1024]{2,1,0:T(8,128)(2,1)}) custom-call(f32[1,4,1024,1024]{3,2,1,0:T(8,128)} %grad.1, f32[4,256,1024]{2,1,0:T(8,128)} %mom.1, f32[4,256,1024]{2,1,0:T(8,128)} %weight.1, f32[4]{0:T(128)} %lr.1, f32[1]{0:T(128)} %bitcast.1.decay), custom_call_target="tpu_custom_call" | custom-call | tf_op jit(solution)/shard_map/muon/pallas_call | solution.py:464
  252.6 0.0 copy-start
  252.6 4.9 %copy.12 = f32[4,256,1024]{2,1,0:T(8,128)} copy(f32[4,256,1024]{2,1,0:T(8,128)} %get-tuple-element.6) | data formatting | bytes 8388608
  257.5 0.0 copy-done
  257.5 2.0 copy.13
  259.5 7.8 %copy.14 = bf16[4,1024,1024]{2,1,0:T(8,128)(2,1)} copy(bf16[4,1024,1024]{2,1,0:T(8,128)(2,1)} %get-tuple-element.8) | data formatting | bytes 16777216
Async XLA Ops:
  252.6 5.0 %copy-start = (f32[4,256,1024]{2,1,0:T(8,128)S(1)}, f32[4,256,1024]{2,1,0:T(8,128)}, u32[]{:S(2)}) copy-start(f32[4,256,1024]{2,1,0:T(8,128)} %get-tuple-element.7) | copy-start | bytes 12582916

commit v4 on v3

--- a/solution.py
+++ b/solution.py
@@ -21,17 +21,26 @@
 BF16 = jnp.bfloat16
 NT = (((1,), (1,)), ((), ()))
 
-ORDER = [(0, 0), (2, 0), (0, 1), (2, 1), (1, 0), (3, 0), (1, 1), (3, 1), (1, 2), (3, 2), (1, 3), (3, 3)]
-PARTS = {0: [(0, 32), (32, 32)], 1: [(0, 32), (32, 16), (48, 8), (56, 8)]}
-MAX_PARTS = 4
-SENT = [3, 4, 5, 6, 7, 8, 9, 10, 12, 12, 12, 12]
-STAGES = {
-    (0, 0): {0: (0, 1), 1: (2, 3), 2: (4, 5), 3: (6, 7), 4: (8,)},
-    (0, 1): {1: (0, 1), 2: (2, 3), 3: (4, 5), 4: (6, 7), 5: (8,)},
-    (1, 0): {4: (0, 1), 5: (2, 3), 6: (4, 5), 7: (6, 7), 8: (8, 9), 9: (10, 11), 10: (12, 13), 11: (14, 15, 16)},
-    (1, 1): {5: (0, 1), 6: (2, 3), 7: (4, 5), 8: (6, 7), 9: (8, 9), 10: (10, 11), 11: (12, 13, 14, 15, 16)},
-}
-HEAD = 5
+ORDER = [(m, p) for p in range(4) for m in (0, 2)] + [(m, p) for p in range(5) for m in (1, 3)]
+PARTS = {0: [(0, 16), (16, 16), (32, 16), (48, 16)], 1: [(0, 16), (16, 16), (32, 16), (48, 8), (56, 8)]}
+MAX_PARTS = 5
+NPIECE = len(ORDER)
+SENT = [k + 3 if k < 14 else NPIECE for k in range(NPIECE)]
+
+
+def stages(core, chip):
+    first, parts = (0, 4) if core == 0 else (8, 5)
+    out = {}
+    for p in range(parts):
+        k = first + 2 * p + chip
+        out.setdefault(k, []).extend((4 * p, 4 * p + 1))
+        out.setdefault(min(k + 1, NPIECE - 1), []).extend((4 * p + 2, 4 * p + 3))
+    out.setdefault(min(k + 2, NPIECE - 1), []).append(4 * parts)
+    return out
+
+
+STAGES = {(core, chip): stages(core, chip) for core in range(2) for chip in range(2)}
+HEAD = 9
 STEP = 32
 
 
@@ -49,7 +58,7 @@
                 mom_new, w_new, wb,
                 own_yp, own_me, recv_a, recv_b, recv_y, momb, ub, x, gram, poly, x5, x5e, wg, xr, ws, wo, ssq,
                 ld_yp, ld_me, ld_mom, sa, ra, sb, rb, sy, ry, su, sm, ru,
-                zs, zf, zr, pw, rw, lw, se, re, sx, rx, sw, rwb, sd, rd, sf, sl_b, sl_n):
+                zs, zf, zr, pw, rw, lw, se, re, sx, rx, sw, rwb, sd, sm2, sf, sl_b, sl_o, sl_n, rd):
     me = lax.axis_index("dp")
     z = lax.axis_index("tp")
     y, c = lax.div(me, 2), lax.rem(me, 2)
@@ -275,21 +284,23 @@
         def _():
             fn()
 
-    def head(k):
-        if k == HEAD:
-            gathers[0][1]()
-            gathers[0][2]()
-
-            def begin():
-                normalize()
-                square()
-            in_middle(begin)
-        if k == HEAD + 1:
-            in_middle(polynomial)
-        if k == HEAD + 2:
-            in_middle(lambda: update(0, TP // 2))
-        if k == npiece - 1:
-            in_middle(lambda: update(TP // 2, TP))
+    def whole(core):
+        gathers[core][1]()
+        gathers[core][2]()
+        in_middle(normalize)
+
+    def poly_and_update():
+        polynomial()
+        update(0, 1)
+
+    head = {
+        HEAD: lambda: whole(0),
+        HEAD + 1: lambda: in_middle(square),
+        HEAD + 2: lambda: in_middle(poly_and_update),
+        HEAD + 3: lambda: in_middle(lambda: update(1, 2)),
+        HEAD + 4: lambda: in_middle(lambda: update(2, 3)),
+        HEAD + 5: lambda: in_middle(lambda: update(3, TP)),
+    }
 
     chip_sum(0)
     chip_sum(1)
@@ -303,14 +314,14 @@
         for j in range(sent, SENT[k]):
             copy_y(j).start()
         sent = SENT[k]
-        for (core, chip), stages in STAGES.items():
-            if k in stages:
+        for (core, chip), todo in STAGES.items():
+            if k in todo:
                 @pl.when(jnp.logical_and(c == core, y == chip))
                 def _():
-                    for t in stages[k]:
+                    for t in todo[k]:
                         gathers[core][0](t)
-        if k in (HEAD, HEAD + 1, HEAD + 2):
-            on_core(0, lambda: head(k))
+        if k in head:
+            on_core(0, head[k])
 
     def copy_w(i):
         return mesh_copy(weight.at[peers[i]], wg.at[i - 1], pw.at[i], rw.at[i], dp=peers[i])
@@ -322,13 +333,7 @@
     for cp in load_w:
         cp.start()
 
-    on_core(0, lambda: head(npiece - 1))
-
-    def catch_up():
-        gathers[1][1]()
-        gathers[1][2]()
-        in_middle(normalize)
-    on_core(1, catch_up)
+    on_core(1, lambda: whole(1))
 
     @pl.when(middle)
     def _():
@@ -342,9 +347,17 @@
             return carry
         lax.fori_loop(1 - c, NS_STEPS, step, 0)
 
-    def copy_e(i):
-        blk = row_block(peers[i])
-        return mesh_copy(x5e.at[blk, :], x5.at[blk, :], se.at[i], re.at[i], tp=end)
+    hrows = rows // 2
+
+    def half_block(r, h):
+        return pl.ds(pl.multiple_of(r * rows + h * hrows, hrows), hrows)
+
+    def half(h):
+        return pl.ds(h * hrows, hrows)
+
+    def copy_e(i, h):
+        blk = half_block(peers[i], h)
+        return mesh_copy(x5e.at[blk, :], x5.at[blk, :], se.at[i, h], re.at[i, h], tp=end)
 
     def last(i, s, dst):
         blk = row_block(peers[i])
@@ -353,20 +366,39 @@
     def apply(w, v, mat):
         return w - lr[mat] * (out_scale * v.astype(F32) + decay[0] * w)
 
-    def each(fn):
-        @pl.loop(0, rows // STEP)
+    def each(h, fn):
+        @pl.loop(0, hrows // STEP)
         def _(i):
-            fn(pl.ds(pl.multiple_of(i * STEP, STEP), STEP))
-
-    def to_partner(src, mat, r, sem):
-        return mesh_copy(src, wb.at[mat, row_block(r), :], sem, rd.at[mat, r], dp=partner)
-
-    sends = []
-    stores = []
-
-    def go(cp, into):
-        cp.start()
-        into.append(cp)
+            fn(pl.multiple_of(h * hrows + i * STEP, STEP))
+
+    def to_partner(src, mat, r, h, sem):
+        return mesh_copy(src, wb.at[mat, half_block(r, h), :], sem, rd.at[mat, r, h], dp=partner)
+
+    def send_x(i, h):
+        return mesh_copy(x5.at[half_block(peers[i], h), :], xr.at[me, half(h), :], sx.at[i, h], rx.at[me, h], dp=peers[i])
+
+    def send_w(i, h):
+        return mesh_copy(ws.at[i, half(h), :], wb.at[me, half_block(peers[i], h), :], sw.at[i, h], rwb.at[me, h], dp=peers[2 + i])
+
+    def share_own(i, h):
+        return to_partner(ws.at[i, half(h), :], me, peers[i], h, sd.at[i, h])
+
+    def share_mine(i, h):
+        return to_partner(wo.at[i, half(h), :], peers[i], me, h, sm2.at[i, h])
+
+    def pass_on(i, h):
+        return to_partner(wb.at[peers[i], half_block(yp, h), :], peers[i], yp, h, sf.at[i, h])
+
+    def store_b(i, h):
+        return pltpu.make_async_copy(ws.at[i, half(h), :], wb.at[me, half_block(peers[i], h), :], sl_b.at[i, h])
+
+    def store_o(i, h):
+        return pltpu.make_async_copy(wo.at[i, half(h), :], wb.at[peers[i], half_block(me, h), :], sl_o.at[i, h])
+
+    def store_n(i, h):
+        return pltpu.make_async_copy(wv.at[i, half(h), :], w_new.at[peers[i], half(h), :], sl_n.at[i, h])
+
+    halves = (0, 1)
 
     for i in (2, 3, 0, 1):
         r = peers[i]
@@ -374,58 +406,76 @@
         @pl.when(middle)
         def _():
             last(i, end, x5e)
-            copy_e(i).start()
+            for h in halves:
+                copy_e(i, h).start()
             last(i, z, x5)
 
-        @pl.when(jnp.logical_not(middle))
-        def _():
-            copy_e(i).wait_recv()
-
-        if i > 0:
-            go(mesh_copy(x5.at[row_block(r), :], xr.at[me], sx.at[i], rx.at[me], dp=r), sends)
         if i == 0:
             load_w[0].wait()
-
-            def own(sl):
-                w = apply(wv[0, sl, :], x5[pl.ds(me * rows + sl.start, STEP), :], me)
-                wv[0, sl, :] = w
-                ws[0, sl, :] = w.astype(BF16)
-            each(own)
-            go(pltpu.make_async_copy(wv.at[0], w_new.at[me], sl_n.at[0]), stores)
         else:
             copy_w(i).wait_recv()
-
-            def rest(sl, i=i, r=r):
-                ws[i, sl, :] = apply(wg[i - 1, sl, :], x5[pl.ds(r * rows + sl.start, STEP), :], me).astype(BF16)
-            each(rest)
-        if i < 2:
-            go(mesh_copy(ws.at[i], wb.at[me, row_block(r), :], sw.at[i], rwb.at[me], dp=peers[2 + i]), sends)
-        if i != 1:
-            go(to_partner(ws.at[i], me, r, sd.at[i]), sends)
-        go(pltpu.make_async_copy(ws.at[i], wb.at[me, row_block(r), :], sl_b.at[i]), stores)
-
-    for i in range(1, DP):
+        for h in halves:
+            @pl.when(jnp.logical_not(middle))
+            def _():
+                copy_e(i, h).wait_recv()
+
+            if i > 0:
+                send_x(i, h).start()
+
+            def rows_of(lo, i=i, r=r):
+                sl = pl.ds(lo, STEP)
+                v = x5[pl.ds(pl.multiple_of(r * rows + lo, STEP), STEP), :]
+                if i == 0:
+                    w = apply(wv[0, sl, :], v, me)
+                    wv[0, sl, :] = w
+                else:
+                    w = apply(wg[i - 1, sl, :], v, me)
+                ws[i, sl, :] = w.astype(BF16)
+            each(h, rows_of)
+            if i < 2:
+                send_w(i, h).start()
+            if i != 1:
+                share_own(i, h).start()
+            store_b(i, h).start()
+            if i == 0:
+                store_n(0, h).start()
+
+    def mine(i):
         mat = peers[i]
         load_w[i].wait()
-        mesh_copy(x5.at[row_block(me), :], xr.at[mat], sx.at[0], rx.at[mat], dp=mat).wait_recv()
-
-        def mine(sl, i=i, mat=mat):
-            w = apply(wv[i, sl, :], xr[mat, sl, :], mat)
-            wv[i, sl, :] = w
-            wo[i, sl, :] = w.astype(BF16)
-        each(mine)
-        if i > 1:
-            go(to_partner(wo.at[i], mat, me, sf.at[i]), sends)
-        go(pltpu.make_async_copy(wv.at[i], w_new.at[mat], sl_n.at[i]), stores)
-        go(pltpu.make_async_copy(wo.at[i], wb.at[mat, row_block(me), :], sl_b.at[DP + i]), stores)
-
-    for i in (2, 3):
-        dst = wb.at[peers[i], row_block(yp), :]
-        mesh_copy(ws.at[0], dst, sw.at[0], rwb.at[peers[i]], dp=peers[i]).wait_recv()
-        go(to_partner(dst, peers[i], yp, sf.at[DP + i]), sends)
-
-    for mat, r in ((partner, partner), (partner, yp), (partner, diag), (yp, partner), (diag, partner), (yp, diag), (diag, diag)):
-        to_partner(ws.at[0], mat, r, sd.at[0]).wait_recv()
+        for h in halves:
+            mesh_copy(x5.at[half_block(me, h), :], xr.at[mat, half(h), :], sx.at[0, h], rx.at[mat, h], dp=mat).wait_recv()
+
+            def rows_of(lo):
+                sl = pl.ds(lo, STEP)
+                w = apply(wv[i, sl, :], xr[mat, sl, :], mat)
+                wv[i, sl, :] = w
+                wo[i, sl, :] = w.astype(BF16)
+            each(h, rows_of)
+            if i > 1:
+                share_mine(i, h).start()
+            store_n(i, h).start()
+            store_o(i, h).start()
+
+    def relay(i):
+        for h in halves:
+            mesh_copy(ws.at[0, half(h), :], wb.at[peers[i], half_block(yp, h), :], sw.at[0, h], rwb.at[peers[i], h],
+                      dp=peers[i]).wait_recv()
+            pass_on(i, h).start()
+
+    def core0_order():
+        mine(2)
+        relay(2)
+        mine(1)
+        mine(3)
+        relay(3)
+
+    def core1_order():
+        mine(1)
+        mine(3)
+        relay(3)
+        mine(2)
+        relay(2)
 
     for k in range(npiece):
         copy_a(k).wait_send()
@@ -436,17 +486,34 @@
         @pl.when(me != ORDER[k][0])
         def _():
             copy_u(k).wait_send()
+    for i in range(1, DP):
+        copy_w(i).wait_send()
+
+    on_core(0, core0_order)
+    on_core(1, core1_order)
+
+    for mat, r in ((partner, partner), (partner, yp), (partner, diag), (yp, partner), (diag, partner), (yp, diag), (diag, diag)):
+        for h in halves:
+            to_partner(ws.at[0, half(h), :], mat, r, h, sd.at[0, h]).wait_recv()
+
     for i in range(DP):
-        if i > 0:
-            copy_w(i).wait_send()
-
-        @pl.when(middle)
-        def _():
-            copy_e(i).wait_send()
-    for cp in sends:
-        cp.wait_send()
-    for cp in stores:
-        cp.wait()
+        for h in halves:
+            @pl.when(middle)
+            def _():
+                copy_e(i, h).wait_send()
+
+            if i > 0:
+                send_x(i, h).wait_send()
+                store_o(i, h).wait()
+            if i < 2:
+                send_w(i, h).wait_send()
+            if i != 1:
+                share_own(i, h).wait_send()
+            if i > 1:
+                share_mine(i, h).wait_send()
+                pass_on(i, h).wait_send()
+            store_b(i, h).wait()
+            store_n(i, h).wait()
 
 
 def muon(grad, mom, weight, lr, decay, out_scale):
@@ -470,16 +537,49 @@
         scratch_shapes=[f32] * 6 + [b16, pltpu.VMEM((all_rows, TP * cols), BF16), square, square, slab, slab,
                                     pltpu.VMEM((DP - 1, rows, cols), F32), b16, b16, b16, pltpu.VMEM((16, TP * cols), F32)]
         + [dma((n,))] * 11 + [dma((DP, MAX_PARTS)), dma((nq,)), dma((nq,)), dma((TP, nq))]
-        + [dma((DP,))] * 9 + [dma((DP,)), dma((DP, DP)), dma((2 * DP,)), dma((2 * DP,)), dma((DP,))],
+        + [dma((DP,))] * 3 + [dma((DP, 2))] * 12 + [dma((DP, DP, 2))],
         compiler_params=pltpu.CompilerParams(collective_id=0, has_side_effects=True, vmem_limit_bytes=67043328),
         name="muon",
     )(grad, mom, weight, lr, decay)
 
 
+def copy_kernel(*refs):
+    n = len(refs) // 4
+    sources, outs, bufs, sems = refs[:n], refs[n:2 * n], refs[2 * n:3 * n], refs[3 * n:]
+    reads, writes = [], []
+    for src, out, buf, sem in zip(sources, outs, bufs, sems):
+        for i in range(src.shape[0]):
+            reads.append(pltpu.make_async_copy(src.at[i], buf.at[i], sem.at[0, i]))
+            writes.append(pltpu.make_async_copy(buf.at[i], out.at[i], sem.at[1, i]))
+    for cp in reads:
+        cp.start()
+    for rd, wr in zip(reads, writes):
+        rd.wait()
+        wr.start()
+    for cp in writes:
+        cp.wait()
+
+
+def results(*arrays):
+    flat = [v.reshape(-1, 256, v.shape[-1]) for v in arrays]
+    hbm = pl.BlockSpec(memory_space=pl.ANY)
+    out = pl.pallas_call(
+        copy_kernel,
+        out_shape=tuple(jax.ShapeDtypeStruct(v.shape, v.dtype) for v in flat),
+        in_specs=[hbm] * len(flat),
+        out_specs=(hbm,) * len(flat),
+        scratch_shapes=[pltpu.VMEM(v.shape, v.dtype) for v in flat]
+        + [pltpu.SemaphoreType.DMA((2, v.shape[0])) for v in flat],
+        compiler_params=pltpu.CompilerParams(vmem_limit_bytes=67043328),
+        name="results",
+    )(*flat)
+    return tuple(o.reshape(v.shape) for o, v in zip(out, arrays))
+
+
 def solution(mesh):
     def local_step(grad, mom, weight, learn_rate, decay_rate):
         out_scale = 0.2 * math.sqrt(max(grad.shape[2], grad.shape[3] * TP))
-        return muon(grad, mom, weight, learn_rate, decay_rate.reshape(1), out_scale)
+        return results(*muon(grad, mom, weight, learn_rate, decay_rate.reshape(1), out_scale))
 
     return jax.shard_map(
         local_step,

time: 267 us -> 255 us (0.955)
  local copies, waits for them, and re-layouts: 14.7 us -> 0 us
    unnamed x5 -> x0, local copies, waits for them, and re-layouts: 14.7 us -> none
    pallas_call x0 -> x1, Pallas kernels: none -> 11.4 us  [results(): pl.pallas_call(copy_kernel, out_shape=tuple((jax.ShapeDtypeStruct(v.shape...]
    pallas_call x1, Pallas kernels: 251 us -> 242 us  [muon(): pl.pallas_call(functools.partial(muon_kernel, out_scale), out_shape=(jax....]
where the time goes in v4:
time: 255 us
  Pallas kernels  253 us (99%)
    pallas_call x1, Pallas kernels, muon(): pl.pallas_call(functools.partial(muon_kernel, out_scale), out_shape=(jax....  242 us
    pallas_call x1, Pallas kernels, results(): pl.pallas_call(copy_kernel, out_shape=tuple((jax.ShapeDtypeStruct(v.shape...  11.4 us

profile of v4, /device:TPU:0, one launch (start us, length us, event | category | flops | bytes accessed | tf_op | source)
XLA Modules:
  0.0 254.7 jit_solution(9804395985934685494)
XLA Ops:
  1.3 241.8 %muon.1 = (f32[4,256,1024]{2,1,0:T(8,128)}, f32[4,256,1024]{2,1,0:T(8,128)}, bf16[4,1024,1024]{2,1,0:T(8,128)(2,1)}) custom-call(f32[1,4,1024,1024]{3,2,1,0:T(8,128)} %grad.1, f32[4,256,1024]{2,1,0:T(8,128)} %mom.1, f32[4,256,1024]{2,1,0:T(8,128)} %weight.1, f32[4]{0:T(128)} %lr.1, f32[1]{0:T(128)} %bitcast.3.decay), custom_call_target="tpu_custom_call" | custom-call | tf_op jit(solution)/shard_map/muon/pallas_call | solution.py:531
  243.1 11.4 %results.1 = (f32[4,256,1024]{2,1,0:T(8,128)}, f32[4,256,1024]{2,1,0:T(8,128)}, bf16[16,256,1024]{2,1,0:T(8,128)(2,1)}) custom-call(f32[4,256,1024]{2,1,0:T(8,128)} %get-tuple-element.9.refs_0_, f32[4,256,1024]{2,1,0:T(8,128)} %get-tuple-element.10.refs_1_, bf16[16,256,1024]{2,1,0:T(8,128)(2,1)} %bitcast.4), custom_call_target="tpu_custom_call" | custom-call | tf_op jit(solution)/shard_map/results/pallas_call | solution.py:566

commit v5 on v4

--- a/solution.py
+++ b/solution.py
@@ -100,32 +100,32 @@
         return buf.at[m, pl.ds(lo, n), :]
 
     def load_yp(k):
-        return pltpu.make_async_copy(grad_rows(yp, k), piece(own_yp, k), ld_yp.at[k])
+        return pltpu.make_async_copy(grad_rows(yp, k), piece(own_yp, k), ld_yp)
 
     def load_me(k):
-        return pltpu.make_async_copy(grad_rows(me, k), piece(own_me, k), ld_me.at[k])
+        return pltpu.make_async_copy(grad_rows(me, k), piece(own_me, k), ld_me)
 
     def load_mom(k):
-        return pltpu.make_async_copy(piece(mom, k), piece(momb, k), ld_mom.at[k])
+        return pltpu.make_async_copy(piece(mom, k), piece(momb, k), ld_mom)
 
     def copy_a(k):
-        return mesh_copy(grad_rows(diag, k), piece(recv_a, k), sa.at[k], ra.at[k], dp=partner)
+        return mesh_copy(grad_rows(diag, k), piece(recv_a, k), sa, ra.at[k], dp=partner)
 
     def copy_b(k):
-        return mesh_copy(grad_rows(partner, k), piece(recv_b, k), sb.at[k], rb.at[k], dp=partner)
+        return mesh_copy(grad_rows(partner, k), piece(recv_b, k), sb, rb, dp=partner)
 
     def copy_y(k):
-        return mesh_copy(piece(own_yp, k), piece(recv_y, k), sy.at[k], ry.at[k], dp=yp)
+        return mesh_copy(piece(own_yp, k), piece(recv_y, k), sy, ry.at[k], dp=yp)
 
     def store_mom(k):
-        return pltpu.make_async_copy(piece(momb, k), piece(mom_new, k), sm.at[k])
+        return pltpu.make_async_copy(piece(momb, k), piece(mom_new, k), sm)
 
     def x_block(r, lo, n, s):
         return x.at[pl.ds(pl.multiple_of(r * rows + lo, 16), n), pl.ds(pl.multiple_of(s * cols, cols), cols)]
 
     def copy_u(k):
         m, p, lo, n = span(k)
-        return mesh_copy(piece(ub, k), x_block(me, lo, n, z), su.at[k], ru.at[me, p], dp=m)
+        return mesh_copy(piece(ub, k), x_block(me, lo, n, z), su, ru.at[me, p], dp=m)
 
     for k in range(npiece):
         load_yp(k).start()
@@ -140,7 +140,8 @@
 
     def chip_sum(k):
         m, _, lo, n = span(k)
-        load_yp(k).wait()
+        if k == 0:
+            pltpu.make_async_copy(own_yp, own_yp, ld_yp).wait()
         copy_a(k).wait_recv()
 
         @pl.loop(0, n // STEP)
@@ -150,9 +151,10 @@
 
     def update_piece(k):
         m, _, lo, n = span(k)
-        load_me(k).wait()
-        copy_b(k).wait_recv()
-        load_mom(k).wait()
+        if k == 0:
+            pltpu.make_async_copy(own_me, own_me, ld_me).wait()
+            pltpu.make_async_copy(momb, momb, ld_mom).wait()
+            mesh_copy(recv_b, recv_b, sb, rb, dp=partner).wait_recv()
         copy_y(k).wait_recv()
 
         @pl.loop(0, n // STEP)
@@ -179,37 +181,37 @@
         def copy_own(q):
             _, lo, n, i = todo[q]
             blk = x_block(peers[i], lo, n, z)
-            return mesh_copy(blk, blk, zs.at[q], zr.at[z, q], tp=nb)
+            return mesh_copy(blk, blk, zs, zr.at[jnp.where(middle, 1, 0), q], tp=nb)
 
         def copy_on(q):
             _, lo, n, i = todo[q]
             blk = x_block(peers[i], lo, n, end)
-            return mesh_copy(blk, blk, zf.at[q], zr.at[end, q], tp=other)
-
-        def landed(q, s):
+            return mesh_copy(blk, blk, zf, zr.at[2, q], tp=other)
+
+        def landed(q, s, kind):
             _, lo, n, i = todo[q]
             blk = x_block(peers[i], lo, n, s)
-            mesh_copy(blk, blk, zs.at[q], zr.at[s, q], tp=nb).wait_recv()
+            mesh_copy(blk, blk, zs, zr.at[kind, q], tp=nb).wait_recv()
 
         def stage(t):
             if t < len(todo):
                 p, lo, n, i = todo[t]
                 if i > 0:
-                    mesh_copy(ub.at[0, pl.ds(0, n), :], x_block(peers[i], lo, n, z), su.at[0], ru.at[peers[i], p],
+                    mesh_copy(ub.at[0, pl.ds(0, n), :], x_block(peers[i], lo, n, z), su, ru.at[peers[i], p],
                               dp=peers[i]).wait_recv()
                 copy_own(t).start()
             if t > 0:
                 @pl.when(middle)
                 def _():
-                    landed(t - 1, end)
+                    landed(t - 1, end, 0)
                     copy_on(t - 1).start()
 
         def finish():
             for q in range(len(todo)):
                 @pl.when(middle)
                 def _():
-                    landed(q, other)
-                    landed(q, far)
+                    landed(q, other, 1)
+                    landed(q, far, 2)
                     _, lo, n, i = todo[q]
                     base = peers[i] * rows + lo
 
@@ -221,12 +223,12 @@
                     ssq[...] = part if q == 0 else ssq[...] + part
 
         def drain():
-            for q in range(len(todo)):
-                copy_own(q).wait_send()
-
-                @pl.when(middle)
-                def _():
-                    copy_on(q).wait_send()
+            slab = x.at[:, pl.ds(0, cols)]
+            mesh_copy(slab, slab, zs, zr.at[0, 0], tp=nb).wait_send()
+
+            @pl.when(middle)
+            def _():
+                mesh_copy(slab, slab, zf, zr.at[0, 0], tp=other).wait_send()
 
         return stage, finish, drain
 
@@ -324,7 +326,7 @@
             on_core(0, head[k])
 
     def copy_w(i):
-        return mesh_copy(weight.at[peers[i]], wg.at[i - 1], pw.at[i], rw.at[i], dp=peers[i])
+        return mesh_copy(weight.at[peers[i]], wg.at[i - 1], pw, rw.at[i], dp=peers[i])
 
     wv = own_me
     load_w = [pltpu.make_async_copy(weight.at[peers[i]], wv.at[i], lw.at[i]) for i in range(DP)]
@@ -357,7 +359,7 @@
 
     def copy_e(i, h):
         blk = half_block(peers[i], h)
-        return mesh_copy(x5e.at[blk, :], x5.at[blk, :], se.at[i, h], re.at[i, h], tp=end)
+        return mesh_copy(x5e.at[blk, :], x5.at[blk, :], se, re.at[i, h], tp=end)
 
     def last(i, s, dst):
         blk = row_block(peers[i])
@@ -371,32 +373,32 @@
         def _(i):
             fn(pl.multiple_of(h * hrows + i * STEP, STEP))
 
-    def to_partner(src, mat, r, h, sem):
-        return mesh_copy(src, wb.at[mat, half_block(r, h), :], sem, rd.at[mat, r, h], dp=partner)
+    def to_partner(src, mat, r, h, sem, slot):
+        return mesh_copy(src, wb.at[mat, half_block(r, h), :], sem, rd.at[slot, h], dp=partner)
 
     def send_x(i, h):
-        return mesh_copy(x5.at[half_block(peers[i], h), :], xr.at[me, half(h), :], sx.at[i, h], rx.at[me, h], dp=peers[i])
+        return mesh_copy(x5.at[half_block(peers[i], h), :], xr.at[me, half(h), :], sx, rx.at[me, h], dp=peers[i])
 
     def send_w(i, h):
-        return mesh_copy(ws.at[i, half(h), :], wb.at[me, half_block(peers[i], h), :], sw.at[i, h], rwb.at[me, h], dp=peers[2 + i])
+        return mesh_copy(ws.at[i, half(h), :], wb.at[me, half_block(peers[i], h), :], sw, rwb.at[me, h], dp=peers[2 + i])
 
     def share_own(i, h):
-        return to_partner(ws.at[i, half(h), :], me, peers[i], h, sd.at[i, h])
+        return to_partner(ws.at[i, half(h), :], me, peers[i], h, sd, (0, None, 1, 2)[i])
 
     def share_mine(i, h):
-        return to_partner(wo.at[i, half(h), :], peers[i], me, h, sm2.at[i, h])
+        return to_partner(wo.at[i, half(h), :], peers[i], me, h, sm2, 1 + i)
 
     def pass_on(i, h):
-        return to_partner(wb.at[peers[i], half_block(yp, h), :], peers[i], yp, h, sf.at[i, h])
+        return to_partner(wb.at[peers[i], half_block(yp, h), :], peers[i], yp, h, sf, 3 + i)
 
     def store_b(i, h):
-        return pltpu.make_async_copy(ws.at[i, half(h), :], wb.at[me, half_block(peers[i], h), :], sl_b.at[i, h])
+        return pltpu.make_async_copy(ws.at[i, half(h), :], wb.at[me, half_block(peers[i], h), :], sl_b)
 
     def store_o(i, h):
-        return pltpu.make_async_copy(wo.at[i, half(h), :], wb.at[peers[i], half_block(me, h), :], sl_o.at[i, h])
+        return pltpu.make_async_copy(wo.at[i, half(h), :], wb.at[peers[i], half_block(me, h), :], sl_o)
 
     def store_n(i, h):
-        return pltpu.make_async_copy(wv.at[i, half(h), :], w_new.at[peers[i], half(h), :], sl_n.at[i, h])
+        return pltpu.make_async_copy(wv.at[i, half(h), :], w_new.at[peers[i], half(h), :], sl_n)
 
     halves = (0, 1)
 
@@ -444,7 +446,7 @@
         mat = peers[i]
         load_w[i].wait()
         for h in halves:
-            mesh_copy(x5.at[half_block(me, h), :], xr.at[mat, half(h), :], sx.at[0, h], rx.at[mat, h], dp=mat).wait_recv()
+            mesh_copy(x5.at[half_block(me, h), :], xr.at[mat, half(h), :], sx, rx.at[mat, h], dp=mat).wait_recv()
 
             def rows_of(lo):
                 sl = pl.ds(lo, STEP)
@@ -459,7 +461,7 @@
 
     def relay(i):
         for h in halves:
-            mesh_copy(ws.at[0, half(h), :], wb.at[peers[i], half_block(yp, h), :], sw.at[0, h], rwb.at[peers[i], h],
+            mesh_copy(ws.at[0, half(h), :], wb.at[peers[i], half_block(yp, h), :], sw, rwb.at[peers[i], h],
                       dp=peers[i]).wait_recv()
             pass_on(i, h).start()
 
@@ -477,43 +479,36 @@
         mine(2)
         relay(2)
 
-    for k in range(npiece):
-        copy_a(k).wait_send()
-        copy_b(k).wait_send()
-        copy_y(k).wait_send()
-        store_mom(k).wait()
-
-        @pl.when(me != ORDER[k][0])
-        def _():
-            copy_u(k).wait_send()
-    for i in range(1, DP):
-        copy_w(i).wait_send()
+    mesh_copy(recv_a, recv_a, sa, ra.at[0], dp=partner).wait_send()
+    mesh_copy(recv_b, recv_b, sb, rb, dp=partner).wait_send()
+    mesh_copy(own_yp, own_yp, sy, ry.at[0], dp=yp).wait_send()
+    pltpu.make_async_copy(momb, momb, sm).wait()
+    mesh_copy(ub.at[1:DP], ub.at[1:DP], su, ru.at[0, 0], dp=partner).wait_send()
+    mesh_copy(wg, wg, pw, rw.at[0], dp=partner).wait_send()
 
     on_core(0, core0_order)
     on_core(1, core1_order)
 
-    for mat, r in ((partner, partner), (partner, yp), (partner, diag), (yp, partner), (diag, partner), (yp, diag), (diag, diag)):
+    arrivals = ((partner, partner), (partner, diag), (partner, yp), (diag, partner), (yp, partner), (diag, diag), (yp, diag))
+    for slot, (mat, r) in enumerate(arrivals):
         for h in halves:
-            to_partner(ws.at[0, half(h), :], mat, r, h, sd.at[0, h]).wait_recv()
-
-    for i in range(DP):
-        for h in halves:
-            @pl.when(middle)
-            def _():
-                copy_e(i, h).wait_send()
-
-            if i > 0:
-                send_x(i, h).wait_send()
-                store_o(i, h).wait()
-            if i < 2:
-                send_w(i, h).wait_send()
-            if i != 1:
-                share_own(i, h).wait_send()
-            if i > 1:
-                share_mine(i, h).wait_send()
-                pass_on(i, h).wait_send()
-            store_b(i, h).wait()
-            store_n(i, h).wait()
+            to_partner(ws.at[0, half(h), :], mat, r, h, sd, slot).wait_recv()
+
+    @pl.when(middle)
+    def _():
+        mesh_copy(x5e, x5e, se, re.at[0, 0], tp=end).wait_send()
+
+    def sent(n, sem, slot):
+        mesh_copy(ws.at[0:n], ws.at[0:n], sem, slot, dp=partner).wait_send()
+
+    sent(3, sx, rx.at[0, 0])
+    sent(2, sw, rwb.at[0, 0])
+    sent(3, sd, rd.at[0, 0])
+    sent(2, sm2, rd.at[0, 0])
+    sent(2, sf, rd.at[0, 0])
+    pltpu.make_async_copy(ws, ws, sl_b).wait()
+    pltpu.make_async_copy(wo.at[1:DP], wo.at[1:DP], sl_o).wait()
+    pltpu.make_async_copy(wv, wv, sl_n).wait()
 
 
 def muon(grad, mom, weight, lr, decay, out_scale):
@@ -536,8 +531,8 @@
         out_specs=[hbm] * 3,
         scratch_shapes=[f32] * 6 + [b16, pltpu.VMEM((all_rows, TP * cols), BF16), square, square, slab, slab,
                                     pltpu.VMEM((DP - 1, rows, cols), F32), b16, b16, b16, pltpu.VMEM((16, TP * cols), F32)]
-        + [dma((n,))] * 11 + [dma((DP, MAX_PARTS)), dma((nq,)), dma((nq,)), dma((TP, nq))]
-        + [dma((DP,))] * 3 + [dma((DP, 2))] * 12 + [dma((DP, DP, 2))],
+        + [dma] * 4 + [dma((n,)), dma, dma, dma, dma((n,)), dma, dma, dma((DP, MAX_PARTS)), dma, dma, dma((3, nq)), dma, dma((DP,)),
+           dma((DP,)), dma, dma((DP, 2)), dma, dma((DP, 2)), dma, dma((DP, 2))] + [dma] * 6 + [dma((7, 2))],
         compiler_params=pltpu.CompilerParams(collective_id=0, has_side_effects=True, vmem_limit_bytes=67043328),
         name="muon",
     )(grad, mom, weight, lr, decay)

time: 255 us -> 253 us (level)
  no operation moved by 1% of the time
where the time goes in v5:
time: 253 us; the launch traced here: 252 us
  Pallas kernels  251 us (99%)
    pallas_call x1, Pallas kernels, muon(): pl.pallas_call(functools.partial(muon_kernel, out_scale), out_shape=(jax....  240 us
    pallas_call x1, Pallas kernels, results(): pl.pallas_call(copy_kernel, out_shape=tuple((jax.ShapeDtypeStruct(v.shape...  11.4 us

profile of v5, /device:TPU:0, one launch (start us, length us, event | category | flops | bytes accessed | tf_op | source)
XLA Modules:
  0.0 252.4 jit_solution(4815781217043131527)
XLA Ops:
  1.3 239.5 %muon.1 = (f32[4,256,1024]{2,1,0:T(8,128)}, f32[4,256,1024]{2,1,0:T(8,128)}, bf16[4,1024,1024]{2,1,0:T(8,128)(2,1)}) custom-call(f32[1,4,1024,1024]{3,2,1,0:T(8,128)} %grad.1, f32[4,256,1024]{2,1,0:T(8,128)} %mom.1, f32[4,256,1024]{2,1,0:T(8,128)} %weight.1, f32[4]{0:T(128)} %lr.1, f32[1]{0:T(128)} %bitcast.3.decay), custom_call_target="tpu_custom_call" | custom-call | tf_op jit(solution)/shard_map/muon/pallas_call | solution.py:526
  240.8 11.4 %results.1 = (f32[4,256,1024]{2,1,0:T(8,128)}, f32[4,256,1024]{2,1,0:T(8,128)}, bf16[16,256,1024]{2,1,0:T(8,128)(2,1)}) custom-call(f32[4,256,1024]{2,1,0:T(8,128)} %get-tuple-element.9.refs_0_, f32[4,256,1024]{2,1,0:T(8,128)} %get-tuple-element.10.refs_1_, bf16[16,256,1024]{2,1,0:T(8,128)(2,1)} %bitcast.4), custom_call_target="tpu_custom_call" | custom-call | tf_op jit(solution)/shard_map/results/pallas_call | solution.py:561

commit v6 on v5

--- a/solution.py
+++ b/solution.py
@@ -100,7 +100,7 @@
         return buf.at[m, pl.ds(lo, n), :]
 
     def load_yp(k):
-        return pltpu.make_async_copy(grad_rows(yp, k), piece(own_yp, k), ld_yp)
+        return pltpu.make_async_copy(grad_rows(yp, k), piece(own_yp, k), ld_yp.at[0 if k < 2 else 1])
 
     def load_me(k):
         return pltpu.make_async_copy(grad_rows(me, k), piece(own_me, k), ld_me)
@@ -129,9 +129,6 @@
 
     for k in range(npiece):
         load_yp(k).start()
-    for k in range(npiece):
-        load_me(k).start()
-        load_mom(k).start()
     pl.semaphore_wait(barrier, 3 + jnp.where(z > 0, 1, 0) + jnp.where(z < TP - 1, 1, 0))
     for k in range(npiece):
         copy_a(k).start()
@@ -141,7 +138,11 @@
     def chip_sum(k):
         m, _, lo, n = span(k)
         if k == 0:
-            pltpu.make_async_copy(own_yp, own_yp, ld_yp).wait()
+            early = own_yp.at[0:2, 0:rows // 4]
+            pltpu.make_async_copy(early, early, ld_yp.at[0]).wait()
+        if k == 2:
+            late = own_yp.at[:, 0:rows - rows // 8]
+            pltpu.make_async_copy(late, late, ld_yp.at[1]).wait()
         copy_a(k).wait_recv()
 
         @pl.loop(0, n // STEP)
@@ -305,9 +306,12 @@
     }
 
     chip_sum(0)
+    copy_y(0).start()
     chip_sum(1)
-    copy_y(0).start()
     copy_y(1).start()
+    for k in range(npiece):
+        load_me(k).start()
+        load_mom(k).start()
     sent = 2
     for k in range(npiece):
         for j in range(sent, SENT[k]):
@@ -531,7 +535,7 @@
         out_specs=[hbm] * 3,
         scratch_shapes=[f32] * 6 + [b16, pltpu.VMEM((all_rows, TP * cols), BF16), square, square, slab, slab,
                                     pltpu.VMEM((DP - 1, rows, cols), F32), b16, b16, b16, pltpu.VMEM((16, TP * cols), F32)]
-        + [dma] * 4 + [dma((n,)), dma, dma, dma, dma((n,)), dma, dma, dma((DP, MAX_PARTS)), dma, dma, dma((3, nq)), dma, dma((DP,)),
+        + [dma((2,)), dma, dma, dma] + [dma((n,)), dma, dma, dma, dma((n,)), dma, dma, dma((DP, MAX_PARTS)), dma, dma, dma((3, nq)), dma, dma((DP,)),
            dma((DP,)), dma, dma((DP, 2)), dma, dma((DP, 2)), dma, dma((DP, 2))] + [dma] * 6 + [dma((7, 2))],
         compiler_params=pltpu.CompilerParams(collective_id=0, has_side_effects=True, vmem_limit_bytes=67043328),
         name="muon",

time: 253 us -> 252 us (level)
  no operation moved by 1% of the time
where the time goes in v6:
time: 252 us
  Pallas kernels  251 us (100%)
    pallas_call x1, Pallas kernels, muon(): pl.pallas_call(functools.partial(muon_kernel, out_scale), out_shape=(jax....  239 us
    pallas_call x1, Pallas kernels, results(): pl.pallas_call(copy_kernel, out_shape=tuple((jax.ShapeDtypeStruct(v.shape...  11.4 us

profile of v6, /device:TPU:0, one launch (start us, length us, event | category | flops | bytes accessed | tf_op | source)
XLA Modules:
  0.0 252.1 jit_solution(5624636343599565783)
XLA Ops:
  1.3 239.2 %muon.1 = (f32[4,256,1024]{2,1,0:T(8,128)}, f32[4,256,1024]{2,1,0:T(8,128)}, bf16[4,1024,1024]{2,1,0:T(8,128)(2,1)}) custom-call(f32[1,4,1024,1024]{3,2,1,0:T(8,128)} %grad.1, f32[4,256,1024]{2,1,0:T(8,128)} %mom.1, f32[4,256,1024]{2,1,0:T(8,128)} %weight.1, f32[4]{0:T(128)} %lr.1, f32[1]{0:T(128)} %bitcast.3.decay), custom_call_target="tpu_custom_call" | custom-call | tf_op jit(solution)/shard_map/muon/pallas_call | solution.py:530
  240.5 11.4 %results.1 = (f32[4,256,1024]{2,1,0:T(8,128)}, f32[4,256,1024]{2,1,0:T(8,128)}, bf16[16,256,1024]{2,1,0:T(8,128)(2,1)}) custom-call(f32[4,256,1024]{2,1,0:T(8,128)} %get-tuple-element.9.refs_0_, f32[4,256,1024]{2,1,0:T(8,128)} %get-tuple-element.10.refs_1_, bf16[16,256,1024]{2,1,0:T(8,128)(2,1)} %bitcast.4), custom_call_target="tpu_custom_call" | custom-call | tf_op jit(solution)/shard_map/results/pallas_call | solution.py:565
